TPU v7x, 32 devices: a whole 2x2x4 slice. The times are simulated.
32 devices in a mesh: dp: 4 (over x, core), wide: 8 (over z, y).
Axes of the slice: x: 2, y: 2, z: 4, core: 2. Of those that a mesh axis runs over, the one named last changes fastest.
Arguments:
- streams: float32 [4, 4096, 2048], P(None, 'dp', 'wide'), may hold values from -8 to 8
- cotangent: float32 [4, 4096, 2048], P(None, 'dp', 'wide'), may hold values from -6 to 6
- w_query: bfloat16 [2048, 2048], P('dp', 'wide'), may hold values from -2 to 2
- w_key: bfloat16 [2048, 2048], P('dp', 'wide'), may hold values from -0.125 to 0.125
- w_value: bfloat16 [2048, 2048], P('dp', 'wide'), may hold values from -0.125 to 0.125
- w_out: bfloat16 [2048, 2048], P('wide', 'dp'), may hold values from -1 to 1
- w_gate: bfloat16 [2048, 8192], P('dp', 'wide'), may hold values from -0.125 to 0.125
- w_up: bfloat16 [2048, 8192], P('dp', 'wide'), may hold values from -0.125 to 0.125
- w_down: bfloat16 [8192, 2048], P('wide', 'dp'), may hold values from -0.0625 to 0.0625
- hyper: float32 [2, 4, 6], replicated, may hold values from 0.1 to 0.6
- doc_ids: int32 [4, 1024], P('dp'), may hold values from 0 to 3, never falling along the last dimension, each value on 1 to 512 neighbouring positions
- span_starts: int32 [4, 2], P('dp'), may hold values from 0 to 768, as said below
- span_lengths: int32 [4, 2], P('dp'), may hold values from 64 to 256
Outputs:
- out_streams: float32 [4, 4096, 2048], P(None, 'dp', 'wide')
- d_streams: float32 [4, 4096, 2048], P(None, 'dp', 'wide')
- grad_query: float32 [2048, 2048], P('dp', 'wide')
- grad_key: float32 [2048, 2048], P('dp', 'wide')
- grad_value: float32 [2048, 2048], P('dp', 'wide')
- grad_out: float32 [2048, 2048], P('wide', 'dp')
- grad_gate: float32 [2048, 8192], P('dp', 'wide')
- grad_up: float32 [2048, 8192], P('dp', 'wide')
- grad_down: float32 [8192, 2048], P('wide', 'dp')
- grad_hyper: float32 [2, 4, 6], replicated
- clip_scale: float32 [16], P('wide')
- query_clipped: float32 [2048, 2048], P('dp', 'wide')
- key_clipped: float32 [2048, 2048], P('dp', 'wide')
Inputs may be any that keep to these rules, and one draw needn't show every extreme that they name: `doc_ids`: each row's document numbers never fall; every document holds 1 to 512 tokens, and one holds exactly 512. `span_starts`: span k of a sequence starts and ends inside the k-th of 2 equal regions of the sequence.
All inputs are finite; a program needn't handle non-finite values.
Results may differ from a plain program's by a relative error of at most 0.018.
Values may be sent and summed in bfloat16 or wider, within the bound.
A program may use at most 192 MiB of HBM per device.

v0:
```python
import math

import jax
import jax.numpy as jnp
from jax import lax
from jax.sharding import PartitionSpec as P

D = 2048
H = 16
CLIP_TAU = 6


EPSILON = 1e-05
MASKED = -1e30


def rope_tables(length, head_size):
    half_size = head_size // 2
    inverse = 10000.0 ** (-2.0 * jnp.arange(half_size, dtype=jnp.float32) / head_size)
    angles = jnp.arange(length, dtype=jnp.float32)[:, None] * inverse[None, :]
    cosine_table = jnp.cos(angles)
    sine_table = jnp.sin(angles)
    return (
        jnp.concatenate([cosine_table, cosine_table], axis=1),
        jnp.concatenate([sine_table, sine_table], axis=1),
    )


def rotate(values, cosine_table, sine_table):
    half_size = values.shape[-1] // 2
    turned = jnp.concatenate([-values[..., half_size:], values[..., :half_size]], axis=-1)
    return values * cosine_table[:, None, :] + turned * sine_table[:, None, :]


def rotate_back(grads, cosine_table, sine_table):
    half_size = grads.shape[-1] // 2
    scaled = grads * sine_table[:, None, :]
    turned = jnp.concatenate([scaled[..., half_size:], -scaled[..., :half_size]], axis=-1)
    return grads * cosine_table[:, None, :] + turned


def mix_inputs(weights_in, stream_set):
    return jnp.sum(weights_in[:, None, None] * stream_set, axis=0)


def mix_streams(matrix, stream_set):
    return jnp.sum(matrix[:, :, None, None] * stream_set[None, :, :, :], axis=1)


def mix_back(matrix, grads):
    return jnp.sum(matrix[:, :, None, None] * grads[:, None, :, :], axis=0)


def hyper_rows(pre_grad, post_grad, mix_grad):
    return jnp.concatenate([pre_grad[:, None], post_grad[:, None], mix_grad], axis=1)


def span_labels(positions, starts, lengths):
    inside = (positions[:, None] >= starts[None, :]) & (
        positions[:, None] < (starts + lengths)[None, :]
    )
    numbers = jnp.arange(1, starts.shape[0] + 1, dtype=jnp.int32)
    return jnp.sum(jnp.where(inside, numbers[None, :], 0), axis=1)


def block_mask(doc_row, labels, start_row, count_rows):
    key_pos = jnp.arange(doc_row.shape[0], dtype=jnp.int32)
    query_pos = start_row + jnp.arange(count_rows, dtype=jnp.int32)
    query_docs = lax.dynamic_slice_in_dim(doc_row, start_row, count_rows)
    query_labels = lax.dynamic_slice_in_dim(labels, start_row, count_rows)
    same_doc = query_docs[:, None] == doc_row[None, :]
    causal = key_pos[None, :] <= query_pos[:, None]
    joint_span = (query_labels[:, None] > 0) & (query_labels[:, None] == labels[None, :])
    return same_doc & (causal | joint_span)


def attend_forward(queries, keys_roped, values, doc_row, starts, lengths, score_scale):
    length, head_count, head_size = queries.shape
    block_rows = min(512, length)
    labels = span_labels(jnp.arange(length, dtype=jnp.int32), starts, lengths)

    def one_block(block_index):
        start_row = block_index * block_rows
        query_rows = lax.dynamic_slice_in_dim(queries, start_row, block_rows, 0)
        scores = (
            jnp.einsum("qhd,khd->hqk", query_rows, keys_roped, preferred_element_type=jnp.float32)
            * score_scale
        )
        allowed = block_mask(doc_row, labels, start_row, block_rows)
        masked = jnp.where(allowed[None, :, :], scores, MASKED)
        largest = jnp.max(masked, axis=2)
        exponent = jnp.exp(masked - largest[:, :, None])
        totals = jnp.sum(exponent, axis=2)
        weights_low = (exponent / totals[:, :, None]).astype(jnp.bfloat16)
        attended = jnp.einsum(
            "hqk,khd->qhd", weights_low, values, preferred_element_type=jnp.float32
        )
        return (attended, largest + jnp.log(totals), jnp.max(largest, axis=1))

    attended, log_sums, block_tops = lax.map(
        one_block, jnp.arange(length // block_rows, dtype=jnp.int32)
    )
    return (attended.reshape(length, head_count, head_size), log_sums, jnp.max(block_tops, axis=0))


def attend_backward(
    queries, keys_roped, values, dout, log_sums, doc_row, starts, lengths, score_scale
):
    length, head_count, head_size = queries.shape
    block_rows = min(512, length)
    labels = span_labels(jnp.arange(length, dtype=jnp.int32), starts, lengths)

    def one_block(carry, inputs):
        key_grad, value_grad = carry
        block_index, log_rows = inputs
        start_row = block_index * block_rows
        query_rows = lax.dynamic_slice_in_dim(queries, start_row, block_rows, 0)
        dout_rows = lax.dynamic_slice_in_dim(dout, start_row, block_rows, 0)
        scores = (
            jnp.einsum("qhd,khd->hqk", query_rows, keys_roped, preferred_element_type=jnp.float32)
            * score_scale
        )
        allowed = block_mask(doc_row, labels, start_row, block_rows)
        masked = jnp.where(allowed[None, :, :], scores, MASKED)
        weights_full = jnp.where(allowed[None, :, :], jnp.exp(masked - log_rows[:, :, None]), 0.0)
        weight_grad = jnp.einsum(
            "qhd,khd->hqk", dout_rows, values, preferred_element_type=jnp.float32
        )
        centre = jnp.sum(weights_full * weight_grad, axis=2, keepdims=True)
        score_grad = (weights_full * (weight_grad - centre)).astype(jnp.bfloat16)
        query_grad = score_scale * jnp.einsum(
            "hqk,khd->qhd", score_grad, keys_roped, preferred_element_type=jnp.float32
        )
        key_grad = key_grad + score_scale * jnp.einsum(
            "hqk,qhd->khd", score_grad, query_rows, preferred_element_type=jnp.float32
        )
        value_grad = value_grad + jnp.einsum(
            "hqk,qhd->khd",
            weights_full.astype(jnp.bfloat16),
            dout_rows,
            preferred_element_type=jnp.float32,
        )
        return ((key_grad, value_grad), query_grad)

    empty_grad = jnp.zeros((length, head_count, head_size), jnp.float32)
    count_blocks = length // block_rows
    (key_grad, value_grad), query_grad = lax.scan(
        one_block, (empty_grad, empty_grad), (jnp.arange(count_blocks, dtype=jnp.int32), log_sums)
    )
    return (query_grad.reshape(length, head_count, head_size), key_grad, value_grad)


def row_sums(first_term, second_term):
    return lax.psum((jnp.sum(first_term, axis=1), jnp.sum(second_term, axis=1)), "wide")


def features(piece):
    return lax.all_gather(piece, "wide", axis=1, tiled=True)


def branch_rows(partial_value):
    return lax.psum_scatter(partial_value, "wide", scatter_dimension=1, tiled=True)


def norm_forward(hidden):
    local_width = hidden.shape[1]
    full_width = local_width * lax.axis_size("wide")
    row_total, squares = row_sums(hidden, hidden * hidden)
    centre = row_total / full_width
    spread = squares / full_width - centre * centre
    inverse = lax.rsqrt(spread + EPSILON)
    normed = (hidden - centre[:, None]) * inverse[:, None]
    return (features(normed.astype(jnp.bfloat16)), normed, inverse)


def norm_backward(partial_value, normed, inverse):
    full_width = partial_value.shape[1]
    grad_rows = lax.psum_scatter(partial_value, "wide", scatter_dimension=1, tiled=True)
    row_total, row_cross = row_sums(grad_rows, grad_rows * normed)
    return inverse[:, None] * (
        grad_rows - row_total[:, None] / full_width - normed * row_cross[:, None] / full_width
    )


def per_device(
    streams,
    cotangent,
    w_query,
    w_key,
    w_value,
    w_out,
    w_gate,
    w_up,
    w_down,
    hyper,
    doc_ids,
    span_starts,
    span_lengths,
):
    seq_count, length = doc_ids.shape
    tokens = streams.shape[1]
    head_size = D // H
    column_count = w_query.shape[1]
    head_count = column_count // head_size
    score_scale = 1.0 / math.sqrt(head_size)
    cosine_table, sine_table = rope_tables(length, head_size)
    shape_heads = (seq_count, length, head_count, head_size)
    attn_pre, attn_post, attn_mix = (hyper[0, :, 0], hyper[0, :, 1], hyper[0, :, 2:])
    ffn_pre, ffn_post, ffn_mix = (hyper[1, :, 0], hyper[1, :, 1], hyper[1, :, 2:])
    query_w, key_w, value_w, out_w = (
        lax.all_gather(w_query, "dp", axis=0, tiled=True),
        lax.all_gather(w_key, "dp", axis=0, tiled=True),
        lax.all_gather(w_value, "dp", axis=0, tiled=True),
        lax.all_gather(w_out, "dp", axis=1, tiled=True),
    )
    gate_w, up_w, down_w = (
        lax.all_gather(w_gate, "dp", axis=0, tiled=True),
        lax.all_gather(w_up, "dp", axis=0, tiled=True),
        lax.all_gather(w_down, "dp", axis=1, tiled=True),
    )
    normed_one, kept_one, inverse_one = norm_forward(mix_inputs(attn_pre, streams))
    query_raw = jnp.dot(normed_one, query_w, preferred_element_type=jnp.float32).reshape(
        shape_heads
    )
    key_raw = jnp.dot(normed_one, key_w, preferred_element_type=jnp.float32).reshape(shape_heads)
    values = (
        jnp.dot(normed_one, value_w, preferred_element_type=jnp.float32)
        .astype(jnp.bfloat16)
        .reshape(shape_heads)
    )
    queries = rotate(query_raw, cosine_table, sine_table).astype(jnp.bfloat16)
    keys_roped = rotate(key_raw, cosine_table, sine_table).astype(jnp.bfloat16)

    def forward_sequence(inputs):
        return attend_forward(
            inputs[0], inputs[1], inputs[2], inputs[3], inputs[4], inputs[5], score_scale
        )

    attended, log_sums, seq_tops = lax.map(
        forward_sequence, (queries, keys_roped, values, doc_ids, span_starts, span_lengths)
    )
    head_top = lax.pmax(jnp.max(seq_tops, axis=0), "dp")
    attended_low = attended.reshape(tokens, column_count).astype(jnp.bfloat16)
    branch_one = branch_rows(jnp.dot(attended_low, out_w, preferred_element_type=jnp.float32))
    after_attn = mix_streams(attn_mix, streams) + attn_post[:, None, None] * branch_one[None, :, :]
    normed_two, kept_two, inverse_two = norm_forward(mix_inputs(ffn_pre, after_attn))
    gate_proj = jnp.dot(normed_two, gate_w, preferred_element_type=jnp.float32)
    up_proj = jnp.dot(normed_two, up_w, preferred_element_type=jnp.float32)
    sigmoid_gate = jax.nn.sigmoid(gate_proj)
    hidden = (gate_proj * sigmoid_gate * up_proj).astype(jnp.bfloat16)
    branch_two = branch_rows(jnp.dot(hidden, down_w, preferred_element_type=jnp.float32))
    out_streams = (
        mix_streams(ffn_mix, after_attn) + ffn_post[:, None, None] * branch_two[None, :, :]
    )
    ffn_post_grad = jnp.sum(cotangent * branch_two[None, :, :], axis=(1, 2))
    ffn_mix_grad = jnp.sum(cotangent[:, None, :, :] * after_attn[None, :, :, :], axis=(2, 3))
    two_grad = features(jnp.sum(ffn_post[:, None, None] * cotangent, axis=0).astype(jnp.bfloat16))
    hidden_grad = jnp.dot(two_grad, down_w.T, preferred_element_type=jnp.float32)
    down_wgrad = jnp.einsum("tf,td->fd", hidden, two_grad, preferred_element_type=jnp.float32)
    gate_grad = (
        hidden_grad * up_proj * sigmoid_gate * (1.0 + gate_proj * (1.0 - sigmoid_gate))
    ).astype(jnp.bfloat16)
    up_grad = (hidden_grad * gate_proj * sigmoid_gate).astype(jnp.bfloat16)
    gate_wgrad = jnp.einsum("td,tf->df", normed_two, gate_grad, preferred_element_type=jnp.float32)
    up_wgrad = jnp.einsum("td,tf->df", normed_two, up_grad, preferred_element_type=jnp.float32)
    gate_shard, up_shard, down_shard = (
        lax.psum_scatter(gate_wgrad, "dp", scatter_dimension=0, tiled=True),
        lax.psum_scatter(up_wgrad, "dp", scatter_dimension=0, tiled=True),
        lax.psum_scatter(down_wgrad, "dp", scatter_dimension=1, tiled=True),
    )
    normed_two_grad = jnp.dot(gate_grad, gate_w.T, preferred_element_type=jnp.float32) + jnp.dot(
        up_grad, up_w.T, preferred_element_type=jnp.float32
    )
    h_two_grad = norm_backward(normed_two_grad, kept_two, inverse_two)
    ffn_pre_grad = jnp.sum(h_two_grad[None, :, :] * after_attn, axis=(1, 2))
    after_grad = mix_back(ffn_mix, cotangent) + ffn_pre[:, None, None] * h_two_grad[None, :, :]
    attn_post_grad = jnp.sum(after_grad * branch_one[None, :, :], axis=(1, 2))
    attn_mix_grad = jnp.sum(after_grad[:, None, :, :] * streams[None, :, :, :], axis=(2, 3))
    one_grad = features(jnp.sum(attn_post[:, None, None] * after_grad, axis=0).astype(jnp.bfloat16))
    attended_grad = jnp.dot(one_grad, out_w.T, preferred_element_type=jnp.float32).astype(
        jnp.bfloat16
    )
    out_wgrad = jnp.einsum("tc,td->cd", attended_low, one_grad, preferred_element_type=jnp.float32)

    def backward_sequence(inputs):
        return attend_backward(
            inputs[0],
            inputs[1],
            inputs[2],
            inputs[3],
            inputs[4],
            inputs[5],
            inputs[6],
            inputs[7],
            score_scale,
        )

    query_grad, key_grad, value_grad = lax.map(
        backward_sequence,
        (
            queries,
            keys_roped,
            values,
            attended_grad.reshape(shape_heads),
            log_sums,
            doc_ids,
            span_starts,
            span_lengths,
        ),
    )
    query_low = (
        rotate_back(query_grad, cosine_table, sine_table)
        .reshape(tokens, column_count)
        .astype(jnp.bfloat16)
    )
    key_low = (
        rotate_back(key_grad, cosine_table, sine_table)
        .reshape(tokens, column_count)
        .astype(jnp.bfloat16)
    )
    value_low = value_grad.reshape(tokens, column_count).astype(jnp.bfloat16)
    query_wgrad = jnp.einsum("td,tc->dc", normed_one, query_low, preferred_element_type=jnp.float32)
    key_wgrad = jnp.einsum("td,tc->dc", normed_one, key_low, preferred_element_type=jnp.float32)
    value_wgrad = jnp.einsum("td,tc->dc", normed_one, value_low, preferred_element_type=jnp.float32)
    normed_one_grad = (
        jnp.dot(query_low, query_w.T, preferred_element_type=jnp.float32)
        + jnp.dot(key_low, key_w.T, preferred_element_type=jnp.float32)
        + jnp.dot(value_low, value_w.T, preferred_element_type=jnp.float32)
    )
    h_one_grad = norm_backward(normed_one_grad, kept_one, inverse_one)
    attn_pre_grad = jnp.sum(h_one_grad[None, :, :] * streams, axis=(1, 2))
    streams_grad = mix_back(attn_mix, after_grad) + attn_pre[:, None, None] * h_one_grad[None, :, :]
    hyper_grad = lax.psum(
        jnp.stack(
            [
                hyper_rows(attn_pre_grad, attn_post_grad, attn_mix_grad),
                hyper_rows(ffn_pre_grad, ffn_post_grad, ffn_mix_grad),
            ]
        ),
        ("dp", "wide"),
    )
    query_shard, key_shard, value_shard, out_shard = (
        lax.psum_scatter(query_wgrad, "dp", scatter_dimension=0, tiled=True),
        lax.psum_scatter(key_wgrad, "dp", scatter_dimension=0, tiled=True),
        lax.psum_scatter(value_wgrad, "dp", scatter_dimension=0, tiled=True),
        lax.psum_scatter(out_wgrad, "dp", scatter_dimension=1, tiled=True),
    )
    clip_scale = jnp.sqrt(CLIP_TAU / jnp.maximum(head_top, CLIP_TAU))
    columns = jnp.repeat(clip_scale, head_size)[None, :]
    return (
        out_streams,
        streams_grad,
        query_shard,
        key_shard,
        value_shard,
        out_shard,
        gate_shard,
        up_shard,
        down_shard,
        hyper_grad,
        clip_scale,
        w_query.astype(jnp.float32) * columns,
        w_key.astype(jnp.float32) * columns,
    )


def solution(mesh):
    return jax.shard_map(
        per_device,
        mesh=mesh,
        in_specs=(
            P(None, "dp", "wide"),
            P(None, "dp", "wide"),
            P("dp", "wide"),
            P("dp", "wide"),
            P("dp", "wide"),
            P("wide", "dp"),
            P("dp", "wide"),
            P("dp", "wide"),
            P("wide", "dp"),
            P(),
            P("dp", None),
            P("dp", None),
            P("dp", None),
        ),
        out_specs=(
            P(None, "dp", "wide"),
            P(None, "dp", "wide"),
            P("dp", "wide"),
            P("dp", "wide"),
            P("dp", "wide"),
            P("wide", "dp"),
            P("dp", "wide"),
            P("dp", "wide"),
            P("wide", "dp"),
            P(),
            P("wide"),
            P("dp", "wide"),
            P("dp", "wide"),
        ),
        check_vma=False,
    )
```

profile of v0, /device:TPU:0, one launch (start us, length us, event | category | flops | bytes accessed | tf_op | source)
XLA Modules:
  0.0 1579.6 jit_solution(8456090871075567823)
XLA Ops:
  8.9 2.8 multiply_reduce_fusion.15
  11.9 23.4 %all-reduce.3 = (f32[1024]{0:T(1024)S(1)}, f32[1024]{0:T(1024)S(1)}) all-reduce(f32[1024]{0:T(1024)S(1)} %multiply_reduce_fusion.20, f32[1024]{0:T(1024)S(1)} %get-tuple-element.312), channel_id=1, replica_groups=mesh['dp'=4,'wide'=8] {'wide'}, use_global_device_ids=true, to_apply=%region_5.6 | all-reduce | flops 2048 | bytes 16384 | tf_op jit(solution)/shard_map/psum | solution.py:154
  39.9 1.9 fusion.52
  42.8 66.4 %all-gather.12.cloned.1.call-done = bf16[1024,2048]{1,0:T(8,128)(2,1)} async-done(((bf16[1024,256]{1,0:T(8,128)(2,1)}), bf16[1024,2048]{1,0:T(8,128)(2,1)}) %all-gather.12.cloned.1.call-update) | async-done | bytes 4194320 | tf_op jit(solution)/shard_map/all_gather | solution.py:158
  109.2 3.8 fusion.60
  114.0 11.6 all-gather.14.cloned.1.call-done
  125.7 3.9 fusion.59
  134.0 9.8 all-gather.18.cloned.1.call-done
  143.8 3.8 convolution_convert_fusion.1
  147.9 14.2 while.53
  162.7 5.9 fusion.46
  169.4 6.0 multiply_reduce_fusion.6
  175.5 141.1 %reduce-scatter.12.cloned.1.call-done = f32[1024,256]{1,0:T(8,128)} async-done(((f32[1024,2048]{1,0:T(8,128)}), f32[1024,256]{1,0:T(8,128)}) %reduce-scatter.12.cloned.1.call-update) | async-done | bytes 1048592 | tf_op jit(solution)/shard_map/reduce_scatter | solution.py:162
  316.6 5.3 multiply_reduce_fusion.13
  322.1 19.7 %all-reduce.2 = (f32[1024]{0:T(1024)S(1)}, f32[1024]{0:T(1024)S(1)}) all-reduce(f32[1024]{0:T(1024)S(1)} %multiply_reduce_fusion.19, f32[1024]{0:T(1024)S(1)} %get-tuple-element.310), channel_id=1, replica_groups=mesh['dp'=4,'wide'=8] {'wide'}, use_global_device_ids=true, to_apply=%region_18.19 | all-reduce | flops 2048 | bytes 16384 | tf_op jit(solution)/shard_map/psum | solution.py:154
  344.6 7.2 all-gather.24.cloned.1.call-done
  351.7 77.3 %all-gather.22.cloned.1.call-done = bf16[1024,2048]{1,0:T(8,128)(2,1)} async-done(((bf16[1024,256]{1,0:T(8,128)(2,1)}), bf16[1024,2048]{1,0:T(8,128)(2,1)}) %all-gather.22.cloned.1.call-update) | async-done | bytes 4194320 | tf_op jit(solution)/shard_map/all_gather | solution.py:158
  429.0 10.0 fusion.61
  439.0 24.3 %all-gather.26.cloned.1.call-done = bf16[2048,1024]{1,0:T(8,128)(2,1)} async-done(((bf16[512,1024]{1,0:T(8,128)(2,1)}), bf16[2048,1024]{1,0:T(8,128)(2,1)}) %all-gather.26.cloned.1.call-update) | async-done | bytes 4194320 | tf_op jit(solution)/shard_map/all_gather | solution.py:218
  463.2 12.1 multiply_convert_fusion.3
  475.3 23.8 %all-gather.28.cloned.1.call-done = bf16[1024,2048]{1,0:T(8,128)(2,1)} async-done(((bf16[1024,512]{1,0:T(8,128)(2,1)}), bf16[1024,2048]{1,0:T(8,128)(2,1)}) %all-gather.28.cloned.1.call-update) | async-done | bytes 4194320 | tf_op jit(solution)/shard_map/all_gather | solution.py:219
  499.1 10.5 fusion.62
  509.8 10.8 multiply_reduce_fusion.1
  520.6 137.2 %reduce-scatter.14.cloned.1.call-done = f32[1024,256]{1,0:T(8,128)} async-done(((f32[1024,2048]{1,0:T(8,128)}), f32[1024,256]{1,0:T(8,128)}) %reduce-scatter.14.cloned.1.call-update) | async-done | bytes 1048592 | tf_op jit(solution)/shard_map/reduce_scatter | solution.py:162
  657.7 8.0 multiply_reduce_fusion.7
  666.2 73.4 %all-gather.30.cloned.1.call-done = bf16[1024,2048]{1,0:T(8,128)(2,1)} async-done(((bf16[1024,256]{1,0:T(8,128)(2,1)}), bf16[1024,2048]{1,0:T(8,128)(2,1)}) %all-gather.30.cloned.1.call-update) | async-done | bytes 4194320 | tf_op jit(solution)/shard_map/all_gather | solution.py:158
  739.7 12.9 multiply_convert_fusion.1
  752.6 7.0 fusion.63
  759.6 6.9 convolution_add_fusion
  766.5 146.1 %reduce-scatter.16.cloned.1.call-done = f32[1024,256]{1,0:T(8,128)} async-done(((f32[1024,2048]{1,0:T(8,128)}), f32[1024,256]{1,0:T(8,128)}) %reduce-scatter.16.cloned.1.call-update) | async-done | bytes 1048592 | tf_op jit(solution)/shard_map/reduce_scatter | solution.py:178
  914.5 19.9 %all-reduce.1 = (f32[1024]{0:T(1024)S(1)}, f32[1024]{0:T(1024)S(1)}) all-reduce(f32[1024]{0:T(1024)S(1)} %get-tuple-element.326, f32[1024]{0:T(1024)S(1)} %get-tuple-element.325), channel_id=1, replica_groups=mesh['dp'=4,'wide'=8] {'wide'}, use_global_device_ids=true, to_apply=%region_26.27 | all-reduce | flops 2048 | bytes 16384 | tf_op jit(solution)/shard_map/psum | solution.py:154
  936.4 8.4 multiply_reduce_fusion.9
  946.1 2.5 copy.81
  948.6 68.3 %all-gather.32.cloned.1.call-done = bf16[1024,2048]{1,0:T(8,128)(2,1)} async-done(((bf16[1024,256]{1,0:T(8,128)(2,1)}), bf16[1024,2048]{1,0:T(8,128)(2,1)}) %all-gather.32.cloned.1.call-update) | async-done | bytes 4194320 | tf_op jit(solution)/shard_map/all_gather | solution.py:158
  1016.9 3.8 convolution_convert_fusion
  1020.6 30.5 %while.54 = (s32[]{:T(128)}, f32[1024,2,128]{0,2,1:T(8,128)S(1)}, f32[1024,2,128]{0,2,1:T(8,128)}, f32[2,512,2,128]{3,1,2,0:T(8,128)}, s32[2]{0:T(128)S(1)}, /*i...) while((s32[]{:T(128)}, f32[1024,2,128]{0,2,1:T(8,128)S(1)}, ...), condition=%wide.region_31.32_spmd.clone.clone, body=%wide.region_29.31_spmd.clone.sunk.clone | while | flops 1357250560 | bytes 90224648 | solution.py:147
  1024.1 2.2 multiply_reduce_fusion.23
  1030.5 2.6 fusion.178
  1033.1 2.6 fusion.177
  1039.2 2.2 multiply_reduce_fusion.23
  1045.6 2.6 fusion.178
  1048.2 3.0 fusion.177
  1052.5 2.0 copy.71
  1061.1 4.5 add_add_fusion
  1065.9 10.6 fusion.71
  1076.6 10.7 fusion.69
  1087.8 10.7 fusion.70
  1098.6 4.8 fusion.67
  1103.5 5.0 fusion.66
  1108.6 5.1 fusion.44
  1113.8 4.9 fusion.68
  1118.8 6.5 pmax.7
  1126.8 9.0 multiply_reduce_fusion.2
  1135.8 76.0 %reduce-scatter.18.cloned.1.call-done = f32[1024,256]{1,0:T(8,128)} async-done(((f32[1024,2048]{1,0:T(8,128)}), f32[1024,256]{1,0:T(8,128)}) %reduce-scatter.18.cloned.1.call-update) | async-done | bytes 1048592 | tf_op jit(solution)/shard_map/reduce_scatter | solution.py:178
  1213.7 19.7 %all-reduce = (f32[1024]{0:T(1024)S(1)}, f32[1024]{0:T(1024)S(1)}) all-reduce(f32[1024]{0:T(1024)S(1)} %get-tuple-element.324, f32[1024]{0:T(1024)S(1)} %get-tuple-element.323), channel_id=1, replica_groups=mesh['dp'=4,'wide'=8] {'wide'}, use_global_device_ids=true, to_apply=%region_36.37 | all-reduce | flops 2048 | bytes 16384 | tf_op jit(solution)/shard_map/psum | solution.py:154
  1235.3 7.2 multiply_reduce_fusion.10
  1242.8 38.0 %psum.71 = f32[2,4,6]{2,1,0:T(4,128)} all-reduce(f32[2,4,6]{2,1,0:T(4,128)S(1)} %pad_maximum_fusion.3), channel_id=1, replica_groups=mesh['dp'=4,'wide'=8] {'dp','wide'}, use_global_device_ids=true, to_apply=%region_50.51 | all-reduce | flops 48 | bytes 384 | tf_op jit(solution)/shard_map/psum | solution.py:333
  1280.8 5.8 reduce-scatter.32.cloned.1.call-done
  1286.6 74.4 %reduce-scatter.28.cloned.1.call-done = f32[512,1024]{1,0:T(8,128)} async-done(((f32[2048,1024]{1,0:T(8,128)}), f32[512,1024]{1,0:T(8,128)}) %reduce-scatter.28.cloned.1.call-update) | async-done | bytes 2097168 | tf_op jit(solution)/shard_map/reduce_scatter | solution.py:267
  1361.1 74.4 %reduce-scatter.30.cloned.1.call-done = f32[512,1024]{1,0:T(8,128)} async-done(((f32[2048,1024]{1,0:T(8,128)}), f32[512,1024]{1,0:T(8,128)}) %reduce-scatter.30.cloned.1.call-update) | async-done | bytes 2097168 | tf_op jit(solution)/shard_map/reduce_scatter | solution.py:268
  1435.5 34.3 %reduce-scatter.22.cloned.1.call-done = f32[512,256]{1,0:T(8,128)} async-done(((f32[2048,256]{1,0:T(8,128)}), f32[512,256]{1,0:T(8,128)}) %reduce-scatter.22.cloned.1.call-update) | async-done | bytes 524304 | tf_op jit(solution)/shard_map/reduce_scatter | solution.py:344
  1469.8 34.2 %reduce-scatter.20.cloned.1.call-done = f32[512,256]{1,0:T(8,128)} async-done(((f32[2048,256]{1,0:T(8,128)}), f32[512,256]{1,0:T(8,128)}) %reduce-scatter.20.cloned.1.call-update) | async-done | bytes 524304 | tf_op jit(solution)/shard_map/reduce_scatter | solution.py:343
  1504.0 34.3 %reduce-scatter.26.cloned.1.call-done = f32[256,512]{1,0:T(8,128)} async-done(((f32[256,2048]{1,0:T(8,128)}), f32[256,512]{1,0:T(8,128)}) %reduce-scatter.26.cloned.1.call-update) | async-done | bytes 524304 | tf_op jit(solution)/shard_map/reduce_scatter | solution.py:346
  1538.3 34.3 %reduce-scatter.24.cloned.1.call-done = f32[512,256]{1,0:T(8,128)} async-done(((f32[2048,256]{1,0:T(8,128)}), f32[512,256]{1,0:T(8,128)}) %reduce-scatter.24.cloned.1.call-update) | async-done | bytes 524304 | tf_op jit(solution)/shard_map/reduce_scatter | solution.py:345
  (262 shorter events, 63.2 us)
Async XLA Ops:
  7.2 35.6 %all-gather.16.cloned.1.call-start = ((), (), s32[]{:S(2)}) async-start(), calls=%async_computation.13 | async-start | bytes 1310720 | tf_op jit(solution)/shard_map/all_gather | solution.py:212
  7.9 101.3 %all-gather.12.cloned.1.call-start = ((), (), s32[]{:S(2)}) async-start(), calls=%async_computation.11 | async-start | bytes 4718592 | tf_op jit(solution)/shard_map/all_gather | solution.py:158
  11.7 30.7 %copy-start.2 = (f32[1024,256]{1,0:T(8,128)}, f32[1024,256]{1,0:T(8,128)S(1)}, u32[]{:S(2)}) copy-start(f32[1024,256]{1,0:T(8,128)S(1)} %get-tuple-element.313) | copy-start | bytes 3145732
  36.0 6.7 copy-start.43
  36.0 6.7 copy-start.46
  37.1 88.5 %all-gather.14.cloned.1.call-start = ((), (), s32[]{:S(2)}) async-start(), calls=%async_computation.12 | async-start | bytes 1310720 | tf_op jit(solution)/shard_map/all_gather | solution.py:211
  37.9 105.9 %all-gather.18.cloned.1.call-start = ((), (), s32[]{:S(2)}) async-start(), calls=%async_computation.14 | async-start | bytes 1310720 | tf_op jit(solution)/shard_map/all_gather | solution.py:213
  38.5 124.2 %all-gather.20.cloned.1.call-start = ((), (), s32[]{:S(2)}) async-start(), calls=%async_computation.15 | async-start | bytes 1310720 | tf_op jit(solution)/shard_map/all_gather | solution.py:214
  39.0 277.5 %reduce-scatter.12.cloned.1.call-start = ((), (), s32[]{:S(2)}) async-start(), calls=%async_computation.16 | async-start | bytes 9437184 | tf_op jit(solution)/shard_map/reduce_scatter | solution.py:162
  42.2 70.7 %copy-start.16 = (f32[1024,128]{1,0:T(8,128)}, f32[1024,128]{1,0:T(8,128)S(1)}, u32[]{:S(2)}) copy-start(f32[1024,128]{1,0:T(8,128)S(1)} %get-tuple-element.422) | copy-start | bytes 1572868
  42.5 902.5 %copy-start.12 = (f32[1024,128]{0,1:T(8,128)}, f32[1024,128]{0,1:T(8,128)S(1)}, u32[]{:S(2)}) copy-start(f32[1024,128]{0,1:T(8,128)S(1)} %copy.61) | copy-start | bytes 1572868
  42.7 87.0 %copy-start.14 = (f32[1024,128]{0,1:T(8,128)}, f32[1024,128]{0,1:T(8,128)S(1)}, u32[]{:S(2)}) copy-start(f32[1024,128]{0,1:T(8,128)S(1)} %copy.62) | copy-start | bytes 1572868
  125.7 4.0 copy-start.22
  125.7 4.0 copy-start.23
  133.9 13.9 copy-start.21
  134.0 13.9 copy-start.29
  162.1 6.5 copy-start.41
  162.6 5.9 copy-start.19
  168.6 183.2 %all-gather.24.cloned.1.call-start = ((), (), s32[]{:S(2)}) async-start(), calls=%async_computation.18 | async-start | bytes 5242880 | tf_op jit(solution)/shard_map/all_gather | solution.py:217
  169.3 259.7 %all-gather.22.cloned.1.call-start = ((), (), s32[]{:S(2)}) async-start(), calls=%async_computation.17 | async-start | bytes 4718592 | tf_op jit(solution)/shard_map/all_gather | solution.py:158
  169.4 6.0 copy-start.35
  343.0 120.2 %all-gather.26.cloned.1.call-start = ((), (), s32[]{:S(2)}) async-start(), calls=%async_computation.19 | async-start | bytes 5242880 | tf_op jit(solution)/shard_map/all_gather | solution.py:218
  343.8 155.4 %all-gather.28.cloned.1.call-start = ((), (), s32[]{:S(2)}) async-start(), calls=%async_computation.20 | async-start | bytes 5242880 | tf_op jit(solution)/shard_map/all_gather | solution.py:219
  344.3 313.4 %reduce-scatter.14.cloned.1.call-start = ((), (), s32[]{:S(2)}) async-start(), calls=%async_computation.21 | async-start | bytes 9437184 | tf_op jit(solution)/shard_map/reduce_scatter | solution.py:162
  509.7 229.9 %all-gather.30.cloned.1.call-start = ((), (), s32[]{:S(2)}) async-start(), calls=%async_computation.22 | async-start | bytes 4718592 | tf_op jit(solution)/shard_map/all_gather | solution.py:158
  665.8 246.9 %reduce-scatter.16.cloned.1.call-start = ((), (), s32[]{:S(2)}) async-start(), calls=%async_computation.23 | async-start | bytes 9437184 | tf_op jit(solution)/shard_map/reduce_scatter | solution.py:178
  739.7 12.9 copy-start.44
  752.6 7.0 copy-start.48
  752.6 7.0 copy-start.45
  766.5 250.4 %all-gather.32.cloned.1.call-start = ((), (), s32[]{:S(2)}) async-start(), calls=%async_computation.24 | async-start | bytes 4718592 | tf_op jit(solution)/shard_map/all_gather | solution.py:158
  944.8 267.0 %reduce-scatter.18.cloned.1.call-start = ((), (), s32[]{:S(2)}) async-start(), calls=%async_computation.25 | async-start | bytes 9437184 | tf_op jit(solution)/shard_map/reduce_scatter | solution.py:178
  1020.7 5.7 copy-start.4
  1020.7 5.7 copy-start.8
  1020.7 5.7 copy-start.10
  1020.7 5.7 copy-start.6
  1028.7 4.4 copy-start.1
  1035.7 5.7 copy-start.4
  1035.7 5.7 copy-start.8
  1035.7 5.7 copy-start.10
  1035.8 5.7 copy-start.6
  1043.8 4.4 copy-start.1
  1048.1 3.0 copy-start.9
  1048.1 3.0 copy-start.11
  1051.1 3.4 copy-start.15
  1051.2 3.7 copy-start.17
  1065.6 221.0 %reduce-scatter.32.cloned.1.call-start = ((), (), s32[]{:S(2)}) async-start(), calls=%async_computation.32 | async-start | bytes 10485760 | tf_op jit(solution)/shard_map/reduce_scatter | solution.py:269
  1076.6 284.5 %reduce-scatter.28.cloned.1.call-start = ((), (), s32[]{:S(2)}) async-start(), calls=%async_computation.30 | async-start | bytes 10485760 | tf_op jit(solution)/shard_map/reduce_scatter | solution.py:267
  1087.3 348.2 %reduce-scatter.30.cloned.1.call-start = ((), (), s32[]{:S(2)}) async-start(), calls=%async_computation.31 | async-start | bytes 10485760 | tf_op jit(solution)/shard_map/reduce_scatter | solution.py:268
  1098.5 371.3 %reduce-scatter.22.cloned.1.call-start = ((), (), s32[]{:S(2)}) async-start(), calls=%async_computation.27 | async-start | bytes 2621440 | tf_op jit(solution)/shard_map/reduce_scatter | solution.py:344
  1103.4 5.2 copy-start.20
  1103.5 400.5 %reduce-scatter.20.cloned.1.call-start = ((), (), s32[]{:S(2)}) async-start(), calls=%async_computation.26 | async-start | bytes 2621440 | tf_op jit(solution)/shard_map/reduce_scatter | solution.py:343
  1108.6 429.7 %reduce-scatter.26.cloned.1.call-start = ((), (), s32[]{:S(2)}) async-start(), calls=%async_computation.29 | async-start | bytes 2621440 | tf_op jit(solution)/shard_map/reduce_scatter | solution.py:346
  1113.7 5.1 copy-start.42
  1113.7 11.6 copy-start.27
  1113.7 11.6 copy-start.28
  1113.7 12.7 copy-start.40
  1113.8 13.0 copy-start.37
  1113.8 13.0 copy-start.36
  1113.8 458.8 %reduce-scatter.24.cloned.1.call-start = ((), (), s32[]{:S(2)}) async-start(), calls=%async_computation.28 | async-start | bytes 2621440 | tf_op jit(solution)/shard_map/reduce_scatter | solution.py:345
  1125.3 10.5 copy-start.47
  1126.8 85.0 %copy-start.3 = (f32[1024,256]{1,0:T(8,128)S(1)}, f32[1024,256]{1,0:T(8,128)}, u32[]{:S(2)}) copy-start(f32[1024,256]{1,0:T(8,128)} %copy-done.2) | copy-start | bytes 3145732
  1126.8 85.0 %copy-start.31 = (f32[1024]{0:T(1024)S(1)}, f32[1024]{0:T(1024)}, u32[]{:S(2)}) copy-start(f32[1024]{0:T(1024)} %copy-done.30) | copy-start | bytes 12292
  1126.8 85.0 %copy-start.33 = (f32[1024]{0:T(1024)S(1)}, f32[1024]{0:T(1024)}, u32[]{:S(2)}) copy-start(f32[1024]{0:T(1024)} %copy-done.32) | copy-start | bytes 12292
  1135.8 99.5 %copy-start.39 = (f32[4]{0:T(128)S(1)}, f32[4]{0:T(128)}, u32[]{:S(2)}) copy-start(f32[4]{0:T(128)} %copy-done.38) | copy-start | bytes 52
  (17 other events, 34.8 us)
Sparse Core Ops, SparseCore 0:
  9.5 19.4 all-gather.15
  37.3 71.8 all-gather.11
  110.8 14.8 all-gather.13
  127.1 16.6 all-gather.17
  145.2 16.6 all-gather.19
  168.7 147.8 reduce-scatter.11
  318.1 33.5 all-gather.23
  354.3 74.6 all-gather.21
  430.6 32.6 all-gather.25
  464.7 34.4 all-gather.27
  509.8 147.8 reduce-scatter.13
  665.9 73.7 all-gather.29
  766.6 146.0 reduce-scatter.15
  945.0 71.8 all-gather.31
  1065.8 146.0 reduce-scatter.17
  1214.8 71.7 reduce-scatter.31
  1289.6 71.3 reduce-scatter.27
  1364.1 71.3 reduce-scatter.29
  1438.6 31.1 reduce-scatter.21
  1472.7 31.1 reduce-scatter.19
  1507.1 31.1 reduce-scatter.25
  1541.4 31.1 reduce-scatter.23
where the time goes:
time: 1590 us; the launch traced here: 1580 us
  waiting for transfers between devices  1160 us (73%)
  matrix products  165 us (10%)
  blocking collectives  127 us (8%)
  other arithmetic  86.2 us (5%)
  local copies, waits for them, and re-layouts  21 us (1%)
    all_gather x4, waiting for transfers between devices, features(): return lax.all_gather(piece, 'wide', axis=1, tiled=True)  285 us
    reduce_scatter x2, waiting for transfers between devices, branch_rows(): lax.psum_scatter(partial_value, 'wide', scatter_dimension=1, tiled=True)  278 us
    reduce_scatter x2, waiting for transfers between devices, norm_backward(): lax.psum_scatter(partial_value, 'wide', scatter_dimension=1, tiled=True)  222 us
    psum x4, blocking collectives, row_sums(): lax.psum((jnp.sum(first_term, axis=1), jnp.sum(second_term, axis=1)), 'wi...  82.8 us
    reduce_scatter x1, waiting for transfers between devices, per_device(): lax.psum_scatter(up_wgrad, 'dp', scatter_dimension=0, tiled=True)  74.4 us
    reduce_scatter x1, waiting for transfers between devices, per_device(): lax.psum_scatter(gate_wgrad, 'dp', scatter_dimension=0, tiled=True)  74.4 us
    psum x1, blocking collectives, per_device(): lax.psum(jnp.stack([hyper_rows(attn_pre_grad, attn_post_grad, attn_mix_gr...  38 us
    reduce_scatter x1, waiting for transfers between devices, per_device(): lax.psum_scatter(out_wgrad, 'dp', scatter_dimension=1, tiled=True)  34.3 us
  transfers between devices with their start and end apart: 22, of which 20 were waited for; matrix products, arithmetic and copies ran while one was open for 10% of the time, Pallas kernels for 0%

commit v1 on v0

--- a/solution.py
+++ b/solution.py
@@ -1,9 +1,12 @@
 import math
+from functools import partial
 
 import jax
 import jax.numpy as jnp
 from jax import lax
 from jax.sharding import PartitionSpec as P
+from jax.experimental import pallas as pl
+from jax.experimental.pallas import tpu as pltpu
 
 D = 2048
 H = 16
@@ -12,6 +15,534 @@
 
 EPSILON = 1e-05
 MASKED = -1e30
+
+BF = jnp.bfloat16
+F32 = jnp.float32
+NZ = 4
+def place(count):
+    w = lax.axis_index("wide")
+    rows_y = count // NZ
+    return w, w // rows_y, w % rows_y
+
+
+def greet(w, count):
+    sem = pltpu.get_barrier_semaphore()
+    for k in range(1, count):
+        pl.semaphore_signal(sem, 1, device_id={"wide": (w + k) % count})
+    pl.semaphore_wait(sem, count - 1)
+
+
+def remote(src, dst, send, recv, target):
+    return pltpu.make_async_remote_copy(src, dst, send, recv, device_id={"wide": target})
+
+
+def dma(*shape):
+    return pltpu.SemaphoreType.DMA(shape)
+
+
+class Gather:
+    def __init__(self, pos, count, chunks, x_ref, g_ref, sems):
+        self.w, self.z, self.y = pos
+        self.count, self.ny = count, count // NZ
+        self.chunks, self.rows = chunks, g_ref.shape[0] // chunks
+        self.x_ref, self.g_ref, self.bw = x_ref, g_ref, x_ref.shape[1]
+        self.up_s, self.dn_s, self.y_s, self.z_r, self.y_r = sems
+
+    @staticmethod
+    def scratch(count, chunks):
+        ny = count // NZ
+        return [
+            dma(NZ, chunks),
+            dma(NZ, chunks),
+            dma(NZ, ny - 1, chunks),
+            dma(NZ, chunks),
+            dma(NZ, ny - 1, chunks),
+        ]
+
+    def block(self, b, c):
+        return self.g_ref.at[
+            pl.ds(c * self.rows, self.rows), pl.ds(pl.multiple_of(b * self.bw, self.bw), self.bw)
+        ]
+
+    def source(self, b, c, own):
+        if own:
+            return self.x_ref.at[pl.ds(c * self.rows, self.rows)]
+        return self.block(b, c)
+
+    def up(self, s, zs, c):
+        b = zs * self.ny + self.y
+        target = (self.z + 1) * self.ny + self.y
+        return remote(
+            self.source(b, c, s == 0), self.block(b, c), self.up_s.at[s, c], self.z_r.at[zs, c], target
+        )
+
+    def down(self, s, zs, c):
+        b = zs * self.ny + self.y
+        target = (self.z - 1) * self.ny + self.y
+        return remote(
+            self.source(b, c, s == 0), self.block(b, c), self.dn_s.at[s, c], self.z_r.at[zs, c], target
+        )
+
+    def side(self, s, zs, k, c):
+        b = zs * self.ny + self.y
+        target = self.z * self.ny + (self.y + k) % self.ny
+        return remote(
+            self.source(b, c, s == 0),
+            self.block(b, c),
+            self.y_s.at[zs, k - 1, c],
+            self.y_r.at[zs, k - 1, c],
+            target,
+        )
+
+    def got(self, zs, c):
+        b = zs * self.ny + self.y
+        remote(self.block(b, c), self.block(b, c), self.up_s.at[0, c], self.z_r.at[zs, c], self.w).wait_recv()
+
+    def got_side(self, zs):
+        for k in range(1, self.ny):
+            b = zs * self.ny + (self.y + self.ny - k) % self.ny
+            for c in range(self.chunks):
+                remote(
+                    self.block(b, c),
+                    self.block(b, c),
+                    self.y_s.at[zs, k - 1, c],
+                    self.y_r.at[zs, k - 1, c],
+                    self.w,
+                ).wait_recv()
+
+    def begin(self, c):
+        @pl.when(self.z < NZ - 1)
+        def _():
+            self.up(0, self.z, c).start()
+
+        @pl.when(self.z > 0)
+        def _():
+            self.down(0, self.z, c).start()
+
+        for k in range(1, self.ny):
+            self.side(0, self.z, k, c).start()
+
+    def place_own(self):
+        self.g_ref[:, pl.ds(pl.multiple_of(self.w * self.bw, self.bw), self.bw)] = self.x_ref[...]
+
+    def step(self, s):
+        for c in range(self.chunks):
+
+            @pl.when(self.z - s >= 0)
+            def _():
+                self.got(self.z - s, c)
+
+                @pl.when(self.z < NZ - 1)
+                def _():
+                    self.up(s, self.z - s, c).start()
+
+                for k in range(1, self.ny):
+                    self.side(s, self.z - s, k, c).start()
+
+            @pl.when(self.z + s < NZ)
+            def _():
+                self.got(self.z + s, c)
+
+                @pl.when(self.z > 0)
+                def _():
+                    self.down(s, self.z + s, c).start()
+
+                for k in range(1, self.ny):
+                    self.side(s, self.z + s, k, c).start()
+
+    def drain(self):
+        for c in range(self.chunks):
+            for s in range(NZ):
+
+                @pl.when((self.z - s >= 0) & (self.z < NZ - 1))
+                def _():
+                    self.up(s, self.z - s, c).wait_send()
+
+                @pl.when((self.z + s < NZ) & (self.z > 0))
+                def _():
+                    self.down(s, self.z + s, c).wait_send()
+
+            for k in range(1, self.ny):
+                self.side(0, self.z, k, c).wait_send()
+            for s in range(1, NZ):
+                for k in range(1, self.ny):
+
+                    @pl.when(self.z - s >= 0)
+                    def _():
+                        self.side(s, self.z - s, k, c).wait_send()
+
+                    @pl.when(self.z + s < NZ)
+                    def _():
+                        self.side(s, self.z + s, k, c).wait_send()
+
+    def rest(self):
+        for s in range(1, NZ):
+            self.step(s)
+        for zs in range(NZ):
+            self.got_side(zs)
+
+
+class Scatter:
+    def __init__(self, pos, count, chunks, part, o_ref, scratch):
+        self.w, self.z, self.y = pos
+        self.count, self.ny = count, count // NZ
+        self.chunks, self.rows = chunks, o_ref.shape[0] // chunks
+        self.part, self.o_ref = part, o_ref
+        (
+            self.acc,
+            self.ysnd,
+            self.yrcv,
+            self.usnd,
+            self.urcv,
+            self.dsnd,
+            self.drcv,
+            self.y_s,
+            self.y_r,
+            self.u_s,
+            self.u_r,
+            self.d_s,
+            self.d_r,
+        ) = scratch
+
+    @staticmethod
+    def scratch(count, chunks, tokens, bw):
+        ny = count // NZ
+        v = pltpu.VMEM
+        rows = tokens // chunks
+        return [
+            v((rows, bw), F32),
+            v((NZ, ny - 1, tokens, bw), BF),
+            v((NZ, ny - 1, tokens, bw), BF),
+            v((NZ, tokens, bw), BF),
+            v((NZ, tokens, bw), BF),
+            v((NZ, tokens, bw), BF),
+            v((NZ, tokens, bw), BF),
+            dma(NZ, ny - 1, chunks),
+            dma(NZ, ny - 1, chunks),
+            dma(NZ, chunks),
+            dma(NZ, chunks),
+            dma(NZ, chunks),
+            dma(NZ, chunks),
+        ]
+
+    def order(self):
+        half = self.z // (NZ // 2)
+        plain = [3, 0, 2, 1]
+        return [q + half * (NZ - 1 - 2 * q) for q in plain]
+
+    def span(self, c):
+        return pl.ds(c * self.rows, self.rows)
+
+    def side(self, zd, k, c):
+        rows = self.span(c)
+        return remote(
+            self.ysnd.at[zd, k - 1, rows],
+            self.yrcv.at[zd, k - 1, rows],
+            self.y_s.at[zd, k - 1, c],
+            self.y_r.at[zd, k - 1, c],
+            self.z * self.ny + (self.y + k) % self.ny,
+        )
+
+    def up(self, zd, c):
+        rows = self.span(c)
+        return remote(
+            self.usnd.at[zd, rows],
+            self.urcv.at[zd, rows],
+            self.u_s.at[zd, c],
+            self.u_r.at[zd, c],
+            (self.z + 1) * self.ny + self.y,
+        )
+
+    def down(self, zd, c):
+        rows = self.span(c)
+        return remote(
+            self.dsnd.at[zd, rows],
+            self.drcv.at[zd, rows],
+            self.d_s.at[zd, c],
+            self.d_r.at[zd, c],
+            (self.z - 1) * self.ny + self.y,
+        )
+
+    def begin(self, c):
+        rows = self.span(c)
+        for zd in self.order():
+            for k in range(1, self.ny):
+                block = zd * self.ny + (self.y + k) % self.ny
+                self.ysnd[zd, k - 1, rows] = self.part(rows, block).astype(BF)
+                self.side(zd, k, c).start()
+
+    def relay(self, c):
+        rows = self.span(c)
+        for zd in self.order():
+            value = self.part(rows, zd * self.ny + self.y)
+            for k in range(1, self.ny):
+                self.side(zd, k, c).wait_recv()
+                value = value + self.yrcv[zd, k - 1, rows].astype(F32)
+            self.acc[...] = value
+
+            @pl.when(zd > self.z)
+            def _():
+                @pl.when(self.z > 0)
+                def _():
+                    self.up(zd, c).wait_recv()
+                    self.acc[...] += self.urcv[zd, rows].astype(F32)
+
+                self.usnd[zd, rows] = self.acc[...].astype(BF)
+                self.up(zd, c).start()
+
+            @pl.when(zd < self.z)
+            def _():
+                @pl.when(self.z < NZ - 1)
+                def _():
+                    self.down(zd, c).wait_recv()
+                    self.acc[...] += self.drcv[zd, rows].astype(F32)
+
+                self.dsnd[zd, rows] = self.acc[...].astype(BF)
+                self.down(zd, c).start()
+
+            @pl.when(zd == self.z)
+            def _():
+                self.o_ref[rows, :] = self.acc[...]
+
+    def finish(self, c):
+        rows = self.span(c)
+
+        @pl.when(self.z > 0)
+        def _():
+            self.up(self.z, c).wait_recv()
+            self.o_ref[rows, :] += self.urcv[self.z, rows].astype(F32)
+
+        @pl.when(self.z < NZ - 1)
+        def _():
+            self.down(self.z, c).wait_recv()
+            self.o_ref[rows, :] += self.drcv[self.z, rows].astype(F32)
+
+    def drain(self):
+        for c in range(self.chunks):
+            for zd in range(NZ):
+                for k in range(1, self.ny):
+                    self.side(zd, k, c).wait_send()
+
+                @pl.when(zd > self.z)
+                def _():
+                    self.up(zd, c).wait_send()
+
+                @pl.when(zd < self.z)
+                def _():
+                    self.down(zd, c).wait_send()
+
+    def run(self):
+        self.begin(0)
+        for c in range(self.chunks):
+            if c + 1 < self.chunks:
+                self.begin(c + 1)
+            self.relay(c)
+        for c in range(self.chunks):
+            self.finish(c)
+
+
+class Totals:
+    def __init__(self, pos, count, own, buf, send, recv):
+        self.w, self.count = pos[0], count
+        self.own, self.buf, self.send, self.recv = own, buf, send, recv
+
+    @staticmethod
+    def scratch(count, tokens):
+        return [
+            pltpu.VMEM((8, tokens), F32),
+            pltpu.VMEM((count, 8, tokens), F32),
+            dma(count - 1),
+            dma(count - 1),
+        ]
+
+    def copy(self, k):
+        return remote(
+            self.own, self.buf.at[k], self.send.at[k - 1], self.recv.at[k - 1], (self.w + k) % self.count
+        )
+
+    def exchange(self, first, second):
+        rows = first.shape[0]
+        lane = lax.broadcasted_iota(jnp.int32, (rows, 128), 1)
+        pair = jnp.where(
+            lane == 0, jnp.broadcast_to(first, (rows, 128)), jnp.broadcast_to(second, (rows, 128))
+        )
+        own = jnp.transpose(pair)[:8]
+        self.own[...] = own
+        for k in range(1, self.count):
+            self.copy(k).start()
+        total = own
+        for k in range(1, self.count):
+            self.copy(k).wait_recv()
+            total = total + self.buf[k]
+        for k in range(1, self.count):
+            self.copy(k).wait_send()
+        return total[0:1], total[1:2]
+
+
+def column(row):
+    return jnp.transpose(jnp.broadcast_to(row, (128, row.shape[1])))
+
+
+def tile_columns(block, bw):
+    return jnp.concatenate([block] * (bw // 128), axis=1)
+
+
+def gather_kernel(count, chunks, x_ref, g_ref, *sems):
+    pos = place(count)
+    greet(pos[0], count)
+    gather = Gather(pos, count, chunks, x_ref, g_ref, sems)
+    for c in range(chunks):
+        gather.begin(c)
+    gather.place_own()
+    gather.rest()
+    gather.drain()
+
+
+def norm_kernel(count, chunks, h_ref, g_ref, n_ref, i_ref, x_ref, own, buf, t_s, t_r, *sems):
+    pos = place(count)
+    greet(pos[0], count)
+    bw = h_ref.shape[1]
+    width = count * bw
+    hidden = h_ref[...]
+    totals = Totals(pos, count, own, buf, t_s, t_r)
+    row_total, squares = totals.exchange(
+        jnp.sum(hidden, axis=1, keepdims=True), jnp.sum(hidden * hidden, axis=1, keepdims=True)
+    )
+    centre = row_total / width
+    inverse = lax.rsqrt(squares / width - centre * centre + EPSILON)
+    inverse_cols = column(inverse)
+    i_ref[...] = inverse_cols
+    normed = (h_ref[...] - tile_columns(column(centre), bw)) * tile_columns(inverse_cols, bw)
+    n_ref[...] = normed
+    x_ref[...] = normed.astype(BF)
+    gather = Gather(pos, count, chunks, x_ref, g_ref, sems)
+    for c in range(chunks):
+        gather.begin(c)
+    gather.place_own()
+    gather.rest()
+    gather.drain()
+
+
+def scatter_kernel(count, chunks, p_ref, o_ref, *scratch):
+    pos = place(count)
+    greet(pos[0], count)
+
+    def part(rows, block):
+        bw = p_ref.shape[1] // count
+        return p_ref[rows, pl.ds(pl.multiple_of(block * bw, bw), bw)].astype(F32)
+
+    scatter = Scatter(pos, count, chunks, part, o_ref, scratch)
+    scatter.run()
+    scatter.drain()
+
+
+def scatter_norm_kernel(count, chunks, p_ref, n_ref, i_ref, o_ref, sum_ref, own, buf, t_s, t_r, *scratch):
+    pos = place(count)
+    greet(pos[0], count)
+    bw = n_ref.shape[1]
+    width = count * bw
+
+    def part(rows, block):
+        bw = p_ref.shape[1] // count
+        return p_ref[rows, pl.ds(pl.multiple_of(block * bw, bw), bw)].astype(F32)
+
+    scatter = Scatter(pos, count, chunks, part, sum_ref, scratch)
+    scatter.run()
+    grads, normed = sum_ref[...], n_ref[...]
+    totals = Totals(pos, count, own, buf, t_s, t_r)
+    row_total, cross = totals.exchange(
+        jnp.sum(grads, axis=1, keepdims=True), jnp.sum(grads * normed, axis=1, keepdims=True)
+    )
+    o_ref[...] = tile_columns(i_ref[...], bw) * (
+        sum_ref[...]
+        - tile_columns(column(row_total / width), bw)
+        - n_ref[...] * tile_columns(column(cross / width), bw)
+    )
+    scatter.drain()
+
+
+VM = pl.BlockSpec(memory_space=pltpu.VMEM)
+
+
+def call(kernel, ident, outs, ins, scratch, name, cost=None):
+    return pl.pallas_call(
+        kernel,
+        out_shape=outs,
+        in_specs=[VM] * len(ins),
+        out_specs=tuple(VM for _ in outs) if isinstance(outs, tuple) else VM,
+        scratch_shapes=scratch,
+        compiler_params=pltpu.CompilerParams(
+            collective_id=ident, has_side_effects=True, vmem_limit_bytes=60 * 1024 * 1024
+        ),
+        name=name,
+        cost_estimate=cost or pl.CostEstimate(flops=40_000_000_000, bytes_accessed=8_000_000, transcendentals=0),
+    )(*ins)
+
+
+AG_CHUNKS = 8
+RS_CHUNKS = 4
+
+
+def features(piece, ident):
+    tokens, bw = piece.shape
+    count = lax.axis_size("wide")
+    return call(
+        partial(gather_kernel, count, AG_CHUNKS),
+        ident,
+        jax.ShapeDtypeStruct((tokens, count * bw), BF),
+        [piece],
+        Gather.scratch(count, AG_CHUNKS),
+        "wide_gather",
+    )
+
+
+def branch_rows(partial_value, ident):
+    tokens = partial_value.shape[0]
+    count = lax.axis_size("wide")
+    bw = partial_value.shape[1] // count
+    return call(
+        partial(scatter_kernel, count, RS_CHUNKS),
+        ident,
+        jax.ShapeDtypeStruct((tokens, bw), F32),
+        [partial_value],
+        Scatter.scratch(count, RS_CHUNKS, tokens, bw),
+        "wide_scatter",
+    )
+
+
+def norm_forward(hidden, ident):
+    tokens, bw = hidden.shape
+    count = lax.axis_size("wide")
+    return call(
+        partial(norm_kernel, count, AG_CHUNKS),
+        ident,
+        (
+            jax.ShapeDtypeStruct((tokens, count * bw), BF),
+            jax.ShapeDtypeStruct((tokens, bw), F32),
+            jax.ShapeDtypeStruct((tokens, 128), F32),
+        ),
+        [hidden],
+        [pltpu.VMEM((tokens, bw), BF)] + Totals.scratch(count, tokens) + Gather.scratch(count, AG_CHUNKS),
+        "norm_gather",
+    )
+
+
+def norm_backward(partial_value, normed, inverse, ident):
+    tokens = partial_value.shape[0]
+    count = lax.axis_size("wide")
+    bw = partial_value.shape[1] // count
+    return call(
+        partial(scatter_norm_kernel, count, RS_CHUNKS),
+        ident,
+        jax.ShapeDtypeStruct((tokens, bw), F32),
+        [partial_value, normed, inverse],
+        [pltpu.VMEM((tokens, bw), F32)] + Totals.scratch(count, tokens) + Scatter.scratch(count, RS_CHUNKS, tokens, bw),
+        "scatter_norm",
+    )
+
+
+def weight_shard(value, axis):
+    return lax.psum_scatter(value.astype(BF), "dp", scatter_dimension=axis, tiled=True).astype(F32)
 
 
 def rope_tables(length, head_size):
@@ -148,38 +679,6 @@
         one_block, (empty_grad, empty_grad), (jnp.arange(count_blocks, dtype=jnp.int32), log_sums)
     )
     return (query_grad.reshape(length, head_count, head_size), key_grad, value_grad)
-
-
-def row_sums(first_term, second_term):
-    return lax.psum((jnp.sum(first_term, axis=1), jnp.sum(second_term, axis=1)), "wide")
-
-
-def features(piece):
-    return lax.all_gather(piece, "wide", axis=1, tiled=True)
-
-
-def branch_rows(partial_value):
-    return lax.psum_scatter(partial_value, "wide", scatter_dimension=1, tiled=True)
-
-
-def norm_forward(hidden):
-    local_width = hidden.shape[1]
-    full_width = local_width * lax.axis_size("wide")
-    row_total, squares = row_sums(hidden, hidden * hidden)
-    centre = row_total / full_width
-    spread = squares / full_width - centre * centre
-    inverse = lax.rsqrt(spread + EPSILON)
-    normed = (hidden - centre[:, None]) * inverse[:, None]
-    return (features(normed.astype(jnp.bfloat16)), normed, inverse)
-
-
-def norm_backward(partial_value, normed, inverse):
-    full_width = partial_value.shape[1]
-    grad_rows = lax.psum_scatter(partial_value, "wide", scatter_dimension=1, tiled=True)
-    row_total, row_cross = row_sums(grad_rows, grad_rows * normed)
-    return inverse[:, None] * (
-        grad_rows - row_total[:, None] / full_width - normed * row_cross[:, None] / full_width
-    )
 
 
 def per_device(
@@ -218,7 +717,7 @@
         lax.all_gather(w_up, "dp", axis=0, tiled=True),
         lax.all_gather(w_down, "dp", axis=1, tiled=True),
     )
-    normed_one, kept_one, inverse_one = norm_forward(mix_inputs(attn_pre, streams))
+    normed_one, kept_one, inverse_one = norm_forward(mix_inputs(attn_pre, streams), 0)
     query_raw = jnp.dot(normed_one, query_w, preferred_element_type=jnp.float32).reshape(
         shape_heads
     )
@@ -241,20 +740,20 @@
     )
     head_top = lax.pmax(jnp.max(seq_tops, axis=0), "dp")
     attended_low = attended.reshape(tokens, column_count).astype(jnp.bfloat16)
-    branch_one = branch_rows(jnp.dot(attended_low, out_w, preferred_element_type=jnp.float32))
+    branch_one = branch_rows(jnp.dot(attended_low, out_w, preferred_element_type=jnp.float32).astype(BF), 1)
     after_attn = mix_streams(attn_mix, streams) + attn_post[:, None, None] * branch_one[None, :, :]
-    normed_two, kept_two, inverse_two = norm_forward(mix_inputs(ffn_pre, after_attn))
+    normed_two, kept_two, inverse_two = norm_forward(mix_inputs(ffn_pre, after_attn), 2)
     gate_proj = jnp.dot(normed_two, gate_w, preferred_element_type=jnp.float32)
     up_proj = jnp.dot(normed_two, up_w, preferred_element_type=jnp.float32)
     sigmoid_gate = jax.nn.sigmoid(gate_proj)
     hidden = (gate_proj * sigmoid_gate * up_proj).astype(jnp.bfloat16)
-    branch_two = branch_rows(jnp.dot(hidden, down_w, preferred_element_type=jnp.float32))
+    branch_two = branch_rows(jnp.dot(hidden, down_w, preferred_element_type=jnp.float32).astype(BF), 3)
     out_streams = (
         mix_streams(ffn_mix, after_attn) + ffn_post[:, None, None] * branch_two[None, :, :]
     )
     ffn_post_grad = jnp.sum(cotangent * branch_two[None, :, :], axis=(1, 2))
     ffn_mix_grad = jnp.sum(cotangent[:, None, :, :] * after_attn[None, :, :, :], axis=(2, 3))
-    two_grad = features(jnp.sum(ffn_post[:, None, None] * cotangent, axis=0).astype(jnp.bfloat16))
+    two_grad = features(jnp.sum(ffn_post[:, None, None] * cotangent, axis=0).astype(BF), 4)
     hidden_grad = jnp.dot(two_grad, down_w.T, preferred_element_type=jnp.float32)
     down_wgrad = jnp.einsum("tf,td->fd", hidden, two_grad, preferred_element_type=jnp.float32)
     gate_grad = (
@@ -264,19 +763,19 @@
     gate_wgrad = jnp.einsum("td,tf->df", normed_two, gate_grad, preferred_element_type=jnp.float32)
     up_wgrad = jnp.einsum("td,tf->df", normed_two, up_grad, preferred_element_type=jnp.float32)
     gate_shard, up_shard, down_shard = (
-        lax.psum_scatter(gate_wgrad, "dp", scatter_dimension=0, tiled=True),
-        lax.psum_scatter(up_wgrad, "dp", scatter_dimension=0, tiled=True),
-        lax.psum_scatter(down_wgrad, "dp", scatter_dimension=1, tiled=True),
+        weight_shard(gate_wgrad, 0),
+        weight_shard(up_wgrad, 0),
+        weight_shard(down_wgrad, 1),
     )
     normed_two_grad = jnp.dot(gate_grad, gate_w.T, preferred_element_type=jnp.float32) + jnp.dot(
         up_grad, up_w.T, preferred_element_type=jnp.float32
     )
-    h_two_grad = norm_backward(normed_two_grad, kept_two, inverse_two)
+    h_two_grad = norm_backward(normed_two_grad.astype(BF), kept_two, inverse_two, 5)
     ffn_pre_grad = jnp.sum(h_two_grad[None, :, :] * after_attn, axis=(1, 2))
     after_grad = mix_back(ffn_mix, cotangent) + ffn_pre[:, None, None] * h_two_grad[None, :, :]
     attn_post_grad = jnp.sum(after_grad * branch_one[None, :, :], axis=(1, 2))
     attn_mix_grad = jnp.sum(after_grad[:, None, :, :] * streams[None, :, :, :], axis=(2, 3))
-    one_grad = features(jnp.sum(attn_post[:, None, None] * after_grad, axis=0).astype(jnp.bfloat16))
+    one_grad = features(jnp.sum(attn_post[:, None, None] * after_grad, axis=0).astype(BF), 6)
     attended_grad = jnp.dot(one_grad, out_w.T, preferred_element_type=jnp.float32).astype(
         jnp.bfloat16
     )
@@ -327,7 +826,7 @@
         + jnp.dot(key_low, key_w.T, preferred_element_type=jnp.float32)
         + jnp.dot(value_low, value_w.T, preferred_element_type=jnp.float32)
     )
-    h_one_grad = norm_backward(normed_one_grad, kept_one, inverse_one)
+    h_one_grad = norm_backward(normed_one_grad.astype(BF), kept_one, inverse_one, 7)
     attn_pre_grad = jnp.sum(h_one_grad[None, :, :] * streams, axis=(1, 2))
     streams_grad = mix_back(attn_mix, after_grad) + attn_pre[:, None, None] * h_one_grad[None, :, :]
     hyper_grad = lax.psum(
@@ -340,10 +839,10 @@
         ("dp", "wide"),
     )
     query_shard, key_shard, value_shard, out_shard = (
-        lax.psum_scatter(query_wgrad, "dp", scatter_dimension=0, tiled=True),
-        lax.psum_scatter(key_wgrad, "dp", scatter_dimension=0, tiled=True),
-        lax.psum_scatter(value_wgrad, "dp", scatter_dimension=0, tiled=True),
-        lax.psum_scatter(out_wgrad, "dp", scatter_dimension=1, tiled=True),
+        weight_shard(query_wgrad, 0),
+        weight_shard(key_wgrad, 0),
+        weight_shard(value_wgrad, 0),
+        weight_shard(out_wgrad, 1),
     )
     clip_scale = jnp.sqrt(CLIP_TAU / jnp.maximum(head_top, CLIP_TAU))
     columns = jnp.repeat(clip_scale, head_size)[None, :]

time: 1590 us -> 825 us (0.52)
  waiting for transfers between devices: 1160 us -> 39.4 us
  Pallas kernels: 0 us -> 447 us
  blocking collectives: 127 us -> 47.5 us
    reduce_scatter x11 -> x7, waiting for transfers between devices: 792 us -> 34.9 us  [weight_shard(): lax.psum_scatter(value.astype(BF), 'dp', scatter_dimension=axis, tiled=True)]
    pallas_call x0 -> x8, Pallas kernels: none -> 447 us  [call(): pl.pallas_call(kernel, out_shape=outs, in_specs=[VM] * len(ins), out_spec...]
    all_gather x4 -> x0, waiting for transfers between devices: 285 us -> none  [features(): return lax.all_gather(piece, 'wide', axis=1, tiled=True)]
    psum x4 -> x0, blocking collectives: 82.8 us -> none  [row_sums(): lax.psum((jnp.sum(first_term, axis=1), jnp.sum(second_term, axis=1)), 'wi...]
    all_gather x1, waiting for transfers between devices: 24.3 us -> 0.01 us  [per_device(): lax.all_gather(w_up, 'dp', axis=0, tiled=True)]
    all_gather x1, waiting for transfers between devices: 23.8 us -> 0.01 us  [per_device(): lax.all_gather(w_down, 'dp', axis=1, tiled=True)]
  transfers between devices with their start and end apart: 22 -> 14, of which waited for: 20 -> 1; matrix products, arithmetic and copies ran while one was open for 10% -> 22% of each run, Pallas kernels for 0% -> 30%
where the time goes in v1:
time: 825 us; the launch traced here: 821 us
  Pallas kernels  447 us (54%)
  matrix products  161 us (20%)
  other arithmetic  89 us (11%)
  blocking collectives  47.5 us (6%)
  waiting for transfers between devices  39.4 us (5%)
  local copies, waits for them, and re-layouts  17.3 us (2%)
  between operations  15.1 us (2%)
    pallas_call x8, Pallas kernels, call(): pl.pallas_call(kernel, out_shape=outs, in_specs=[VM] * len(ins), out_spec...  447 us
    psum x1, blocking collectives, per_device(): lax.psum(jnp.stack([hyper_rows(attn_pre_grad, attn_post_grad, attn_mix_gr...  41.7 us
    reduce_scatter x7, waiting for transfers between devices, weight_shard(): lax.psum_scatter(value.astype(BF), 'dp', scatter_dimension=axis, tiled=True)  34.9 us
  transfers between devices with their start and end apart: 14, of which 1 were waited for; matrix products, arithmetic and copies ran while one was open for 22% of the time, Pallas kernels for 30%

profile of v1, /device:TPU:0, one launch (start us, length us, event | category | flops | bytes accessed | tf_op | source)
XLA Modules:
  0.0 820.6 jit_solution(8711451320223946041)
XLA Ops:
  14.3 3.6 multiply_reduce_fusion.14.h_ref
  17.9 64.9 %norm_gather.2 = (bf16[1024,2048]{1,0:T(8,128)(2,1)}, f32[1024,256]{1,0:T(8,128)}, f32[1024,128]{1,0:T(8,128)}) custom-call(f32[1024,256]{1,0:T(8,128)} %multiply_reduce_fusion.14.h_ref), custom_call_target="tpu_custom_call" | custom-call | flops 40000000000 | bytes 8000000 | tf_op jit(solution)/shard_map/norm_gather/pallas_call | solution.py:468
  82.8 1.9 fusion.48
  85.5 6.0 multiply_reduce_fusion.6
  91.7 4.5 fusion.54
  97.2 3.9 fusion.53
  102.5 3.8 convolution_convert_fusion.10
  106.6 14.0 %while.53 = (s32[]{:T(128)}, bf16[2,512,2,128]{3,1,2,0:T(8,128)(2,1)S(1)}, f32[2,2,512]{2,1,0:T(2,128)S(1)}, f32[2,2]{1,0:T(2,128)S(1)}, s32[2]{0:T(128)S(1)}, /...) while((s32[]{:T(128)}, ...), condition=%wide.region_7.8_spmd.clone, body=%wide.region_3.7_spmd.sunk.clone | while | flops 553648128 | bytes 16573659 | solution.py:631
  110.3 1.5 fusion.150
  111.9 1.8 fusion.151
  118.7 1.8 fusion.151
  121.2 4.7 convolution_convert_fusion.p_ref
  125.9 59.0 %wide_scatter.2 = f32[1024,256]{1,0:T(8,128)} custom-call(bf16[1024,2048]{1,0:T(8,128)(2,1)} %convolution_convert_fusion.p_ref), custom_call_target="tpu_custom_call" | custom-call | flops 40000000000 | bytes 8000000 | tf_op jit(solution)/shard_map/wide_scatter/pallas_call | solution.py:468
  185.0 4.4 multiply_reduce_fusion.13
  189.4 9.6 %multiply_reduce_fusion.1 = (f32[4,4]{1,0:T(4,128)}, f32[4,1024,256]{2,1,0:T(8,128)}, f32[4,1024,256]{2,1,0:T(8,128)}) fusion(f32[4,1024,256]{2,1,0:T(8,128)S(1)} %copy-done.12, f32[4,1024,256]{2,1,0:T(8,128)S(1)} %get-tuple-element.385, f32[4,4]{1,0:T(4,128)S(1)} %copy-done.42), kind=kLoop, calls=%fused_computation.48 | loop fusion | flops 23068656 | bytes 16777344 | tf_op jit(solution)/shard_map/reduce_sum | solution.py:755
  199.0 56.8 %norm_gather.3 = (bf16[1024,2048]{1,0:T(8,128)(2,1)}, f32[1024,256]{1,0:T(8,128)}, f32[1024,128]{1,0:T(8,128)}) custom-call(f32[1024,256]{1,0:T(8,128)} %get-tuple-element.384.h_ref), custom_call_target="tpu_custom_call" | custom-call | flops 40000000000 | bytes 8000000 | tf_op jit(solution)/shard_map/norm_gather/pallas_call | solution.py:468
  255.8 10.0 %fusion.55 = f32[1024,1024]{1,0:T(8,128)} fusion(bf16[1024,2048]{1,0:T(8,128)(2,1)} %get-tuple-element.205, bf16[2048,1024]{1,0:T(8,128)(2,1)} %all-gather.16.cloned.1.call-done), kind=kOutput, calls=%fused_computation.138 | convolution fusion | flops 4294967296 | bytes 12582912 | tf_op jit(solution)/shard_map/dot_general | solution.py:746
  265.8 11.4 %multiply_convert_fusion.3 = (bf16[1024,1024]{1,0:T(8,128)(2,1)S(1)}, f32[1024,1024]{1,0:T(8,128)}) fusion(f32[1024,1024]{1,0:T(8,128)} %fusion.55, bf16[1024,2048]{1,0:T(8,128)(2,1)} %get-tuple-element.205, bf16[2048,1024]{1,0:T(8,128)(2,1)} %all-gather.18.cloned.1.call-done), kind=kOutput, calls=%fused_computation.67 | convolution fusion | flops 4301258752 | bytes 18874368 | tf_op jit(solution)/shard_map/dot_general | solution.py:747
  277.2 8.9 %convolution_convert_fusion.4.p_ref = bf16[1024,2048]{1,0:T(8,128)(2,1)} fusion(bf16[1024,1024]{1,0:T(8,128)(2,1)S(1)} %get-tuple-element.412, bf16[1024,2048]{1,0:T(8,128)(2,1)} %all-gather.20.cloned.1.call-done), kind=kOutput, calls=%fused_computation.76 | convolution fusion | flops 4297064448 | bytes 10485760 | tf_op jit(solution)/shard_map/dot_general | solution.py:750
  286.2 56.3 %wide_scatter.3 = f32[1024,256]{1,0:T(8,128)} custom-call(bf16[1024,2048]{1,0:T(8,128)(2,1)} %convolution_convert_fusion.4.p_ref), custom_call_target="tpu_custom_call" | custom-call | flops 40000000000 | bytes 8000000 | tf_op jit(solution)/shard_map/wide_scatter/pallas_call | solution.py:468
  342.5 8.0 multiply_reduce_fusion.7
  350.5 43.9 %wide_gather.2 = bf16[1024,2048]{1,0:T(8,128)(2,1)} custom-call(bf16[1024,256]{1,0:T(8,128)(2,1)} %get-tuple-element.327.x_ref), custom_call_target="tpu_custom_call" | custom-call | flops 40000000000 | bytes 8000000 | tf_op jit(solution)/shard_map/wide_gather/pallas_call | solution.py:468
  394.4 11.6 %multiply_convert_fusion.1 = (bf16[1024,1024]{1,0:T(8,128)(2,1)S(1)}, bf16[1024,1024]{1,0:T(8,128)(2,1)S(1)}) fusion(f32[1024,1024]{1,0:T(8,128)} %fusion.55, f32[1024,1024]{1,0:T(8,128)} %get-tuple-element.413, bf16[1024,2048]{1,0:T(8,128)(2,1)} %wide_gather.2, bf16[1024,2048]{1,0:T(8,128)(2,1)} %all-gather.20.cloned.1.call-done), kind=kOutput, calls=%fused_computation.63 | convolution fusion | flops 4308598784 | bytes 20971520 | tf_op jit(solution)/shard_map/dot_general | solution.py:757
  406.0 4.5 fusion.56
  410.6 6.1 add_convert_fusion.1.p_ref
  416.7 60.5 %scatter_norm.2 = f32[1024,256]{1,0:T(8,128)} custom-call(bf16[1024,2048]{1,0:T(8,128)(2,1)} %add_convert_fusion.1.p_ref, f32[1024,256]{1,0:T(8,128)} %get-tuple-element.206.n_ref, f32[1024,128]{1,0:T(8,128)} %get-tuple-element.207.i_ref), custom_call_target="tpu_custom_call" | custom-call | flops 40000000000 | bytes 8000000 | tf_op jit(solution)/shard_map/scatter_norm/pallas_call | solution.py:468
  477.2 8.3 %multiply_reduce_fusion.9 = (f32[4]{0:T(128)}, bf16[1024,256]{1,0:T(8,128)(2,1)}, f32[4,1024,256]{2,1,0:T(8,128)}, f32[4]{0:T(128)}) fusion(f32[1024,256]{1,0:T(8,128)S(1)} %copy-done.21, f32[4]{0:T(128)S(1)} %copy-done.44, f32[4,1024,256]{2,1,0:T(8,128)} %get-tuple-element.330, f32[1024,256]{1,0:T(8,128)} %scatter_norm.2, f32[4]{0:T(128)S(1)} %copy-done.46, ...), kind=kLoop, calls=%fused_computation.58 | loop fusion | flops 8126456 | bytes 15204416 | tf_op jit(solution)/shard_map/reduce_sum | solution.py:776
  485.6 36.4 %wide_gather.3 = bf16[1024,2048]{1,0:T(8,128)(2,1)} custom-call(bf16[1024,256]{1,0:T(8,128)(2,1)} %get-tuple-element.323.x_ref), custom_call_target="tpu_custom_call" | custom-call | flops 40000000000 | bytes 8000000 | tf_op jit(solution)/shard_map/wide_gather/pallas_call | solution.py:468
  522.0 3.9 convolution_convert_fusion.9
  526.0 31.6 %while.54 = (s32[]{:T(128)}, f32[1024,2,128]{0,2,1:T(8,128)S(1)}, f32[1024,2,128]{0,2,1:T(8,128)}, f32[2,512,2,128]{3,1,2,0:T(8,128)}, s32[2]{0:T(128)S(1)}, /*i...) while((s32[]{:T(128)}, f32[1024,2,128]{0,2,1:T(8,128)S(1)}, ...), condition=%wide.region_16.17_spmd.clone.clone, body=%wide.region_14.16_spmd.clone.sunk.clone | while | flops 1357250560 | bytes 81835944 | solution.py:678
  529.3 3.0 multiply_reduce_fusion.17
  532.3 2.0 copy-done
  534.7 1.8 fusion.163
  536.5 2.6 fusion.165
  539.0 2.6 fusion.164
  544.9 3.0 multiply_reduce_fusion.17
  547.9 2.0 copy-done
  550.3 1.8 fusion.163
  552.1 2.5 fusion.165
  554.6 2.9 fusion.164
  560.1 2.4 convolution_convert_fusion.7
  562.6 4.5 convolution_convert_fusion.5
  568.5 1.6 copy.81
  573.7 2.4 convolution_convert_fusion.8
  577.4 4.7 convolution_convert_fusion.6
  582.1 9.4 %convolution_convert_fusion.1 = bf16[1024,2048]{1,0:T(8,128)(2,1)} fusion(bf16[1024,1024]{1,0:T(8,128)(2,1)} %copy-done.62, bf16[1024,2048]{1,0:T(8,128)(2,1)} %wide_gather.2), kind=kOutput, calls=%fused_computation.73 | convolution fusion | flops 4297064448 | bytes 10485760 | tf_op jit(solution)/shard_map/tf,td->fd/dot_general | solution.py:758
  592.0 9.5 %convolution_convert_fusion.3 = bf16[2048,1024]{1,0:T(8,128)(2,1)} fusion(bf16[1024,2048]{1,0:T(8,128)(2,1)} %get-tuple-element.205, bf16[1024,1024]{1,0:T(8,128)(2,1)} %copy-done.63), kind=kOutput, calls=%fused_computation.75 | convolution fusion | flops 4297064448 | bytes 10485760 | tf_op jit(solution)/shard_map/td,tf->df/dot_general | solution.py:763
  601.5 9.4 %convolution_convert_fusion.2 = bf16[2048,1024]{1,0:T(8,128)(2,1)} fusion(bf16[1024,2048]{1,0:T(8,128)(2,1)} %get-tuple-element.205, bf16[1024,1024]{1,0:T(8,128)(2,1)} %copy-done.64), kind=kOutput, calls=%fused_computation.74 | convolution fusion | flops 4297064448 | bytes 10485760 | tf_op jit(solution)/shard_map/td,tf->df/dot_general | solution.py:764
  611.7 5.8 pmax.7
  618.7 4.6 fusion.58
  623.3 4.5 fusion.57
  627.8 7.9 multiply_reduce_fusion.2
  635.7 9.2 %add_convert_fusion.p_ref = bf16[1024,2048]{1,0:T(8,128)(2,1)} fusion(f32[1024,2048]{1,0:T(8,128)} %fusion.57, f32[1024,2048]{1,0:T(8,128)} %fusion.58, bf16[1024,256]{0,1:T(8,128)(2,1)S(1)} %bitcast.197, bf16[2048,256]{1,0:T(8,128)(2,1)S(1)} %copy-done.31), kind=kOutput, calls=%fused_computation.54 | convolution fusion | flops 1080033280 | bytes 22544384 | tf_op jit(solution)/shard_map/dot_general | solution.py:827
  644.9 69.3 %scatter_norm.3 = f32[1024,256]{1,0:T(8,128)} custom-call(bf16[1024,2048]{1,0:T(8,128)(2,1)} %add_convert_fusion.p_ref, f32[1024,256]{1,0:T(8,128)} %get-tuple-element.212.n_ref, f32[1024,128]{1,0:T(8,128)} %get-tuple-element.213.i_ref), custom_call_target="tpu_custom_call" | custom-call | flops 40000000000 | bytes 8000000 | tf_op jit(solution)/shard_map/scatter_norm/pallas_call | solution.py:468
  714.3 6.7 multiply_reduce_fusion.10
  721.6 41.7 %psum.7 = f32[2,4,6]{2,1,0:T(4,128)} all-reduce(f32[2,4,6]{2,1,0:T(4,128)S(1)} %pad_maximum_fusion.3), channel_id=1, replica_groups=mesh['dp'=4,'wide'=8] {'dp','wide'}, use_global_device_ids=true, to_apply=%region_30.31 | all-reduce | flops 48 | bytes 384 | tf_op jit(solution)/shard_map/psum | solution.py:832
  763.2 1.8 convert_element_type.146
  765.0 1.8 convert_element_type.150
  766.8 1.8 convert_element_type.144
  768.6 1.8 convert_element_type.148
  770.4 2.8 convert_element_type.156
  773.2 2.9 convert_element_type.152
  776.2 34.9 %reduce-scatter.18.cloned.1.call-done = bf16[512,1024]{1,0:T(8,128)(2,1)} async-done(((bf16[2048,1024]{1,0:T(8,128)(2,1)}), bf16[512,1024]{1,0:T(8,128)(2,1)}) %reduce-scatter.18.cloned.1.call-update) | async-done | bytes 1048592 | tf_op jit(solution)/shard_map/reduce_scatter | solution.py:545
  811.1 2.8 convert_element_type.154
  (261 shorter events, 36.3 us)
Async XLA Ops:
  7.2 5.6 copy-start.38
  7.2 84.5 %all-gather.10.cloned.1.call-start = ((), (), s32[]{:S(2)}) async-start(), calls=%async_computation.8 | async-start | bytes 1310720 | tf_op jit(solution)/shard_map/all_gather | solution.py:711
  7.9 89.3 %all-gather.8.cloned.1.call-start = ((), (), s32[]{:S(2)}) async-start(), calls=%async_computation.7 | async-start | bytes 1310720 | tf_op jit(solution)/shard_map/all_gather | solution.py:710
  8.7 93.8 %all-gather.12.cloned.1.call-start = ((), (), s32[]{:S(2)}) async-start(), calls=%async_computation.9 | async-start | bytes 1310720 | tf_op jit(solution)/shard_map/all_gather | solution.py:712
  9.4 111.8 %all-gather.14.cloned.1.call-start = ((), (), s32[]{:S(2)}) async-start(), calls=%async_computation.10 | async-start | bytes 1310720 | tf_op jit(solution)/shard_map/all_gather | solution.py:713
  10.0 245.8 %all-gather.16.cloned.1.call-start = ((), (), s32[]{:S(2)}) async-start(), calls=%async_computation.11 | async-start | bytes 5242880 | tf_op jit(solution)/shard_map/all_gather | solution.py:716
  10.6 255.2 %all-gather.18.cloned.1.call-start = ((), (), s32[]{:S(2)}) async-start(), calls=%async_computation.12 | async-start | bytes 5242880 | tf_op jit(solution)/shard_map/all_gather | solution.py:717
  11.1 266.1 %all-gather.20.cloned.1.call-start = ((), (), s32[]{:S(2)}) async-start(), calls=%async_computation.13 | async-start | bytes 5242880 | tf_op jit(solution)/shard_map/all_gather | solution.py:718
  11.9 751.3 %reduce-scatter.10.cloned.1.call-start = ((), (), s32[]{:S(2)}) async-start(), calls=%async_computation.15 | async-start | bytes 1310720 | tf_op jit(solution)/shard_map/reduce_scatter | solution.py:545
  13.6 69.2 %copy-start.47 = (f32[4]{0:T(128)}, f32[4]{0:T(128)S(1)}, u32[]{:S(2)}) copy-start(f32[4]{0:T(128)S(1)} %get-tuple-element.332) | copy-start | bytes 52
  14.3 71.3 %copy-start.39 = (f32[4,4]{1,0:T(4,128)}, f32[4,4]{1,0:T(4,128)S(1)}, u32[]{:S(2)}) copy-start(f32[4,4]{1,0:T(4,128)S(1)} %get-tuple-element.407) | copy-start | bytes 196
  85.1 6.5 copy-start.18
  85.3 15.9 %copy-start.15 = (f32[1024,128]{0,1:T(8,128)}, f32[1024,128]{0,1:T(8,128)S(1)}, u32[]{:S(2)}) copy-start(f32[1024,128]{0,1:T(8,128)S(1)} %copy.61) | copy-start | bytes 1572868
  85.5 15.7 %copy-start.17 = (f32[1024,128]{0,1:T(8,128)}, f32[1024,128]{0,1:T(8,128)S(1)}, u32[]{:S(2)}) copy-start(f32[1024,128]{0,1:T(8,128)S(1)} %copy.62) | copy-start | bytes 1572868
  85.5 6.0 copy-start.55
  85.5 6.0 copy-start.58
  97.2 4.0 copy-start.26
  102.4 4.2 copy-start.24
  102.4 4.2 copy-start.34
  120.5 5.3 copy-start.5
  120.6 5.3 copy-start.6
  120.6 5.3 copy-start.9
  120.6 5.3 copy-start.27
  120.6 5.3 copy-start.36
  120.6 5.3 copy-start.53
  121.2 63.8 %copy-start.22 = (bf16[2,512,2,128]{3,2,1,0:T(2,128)(2,1)}, bf16[2,512,2,128]{3,2,1,0:T(2,128)(2,1)S(1)}, u32[]{:S(2)}) copy-start(bf16[2,512,2,128]{3,2,1,0:T(2,128)(2,1)S(1)} %copy.66) | copy-start | bytes 1572868
  125.9 59.0 %copy-start.43 = (f32[4]{0:T(128)S(1)}, f32[4]{0:T(128)}, u32[]{:S(2)}) copy-start(f32[4]{0:T(128)} %get-tuple-element.333) | copy-start | bytes 52
  125.9 59.0 %copy-start.45 = (f32[4]{0:T(128)S(1)}, f32[4]{0:T(128)}, u32[]{:S(2)}) copy-start(f32[4]{0:T(128)} %get-tuple-element.334) | copy-start | bytes 52
  184.9 4.5 copy-start.12
  185.0 4.4 copy-start.42
  189.4 9.6 %copy-start.4 = (f32[4,1024,256]{2,1,0:T(8,128)}, f32[4,1024,256]{2,1,0:T(8,128)S(1)}, u32[]{:S(2)}) copy-start(f32[4,1024,256]{2,1,0:T(8,128)S(1)} %get-tuple-element.385) | copy-start | bytes 12582916
  277.2 9.0 %copy-start.62 = (bf16[1024,1024]{1,0:T(8,128)(2,1)}, bf16[1024,1024]{1,0:T(8,128)(2,1)S(1)}, u32[]{:S(2)}) copy-start(bf16[1024,1024]{1,0:T(8,128)(2,1)S(1)} %get-tuple-element.412) | copy-start | bytes 6291460
  286.2 56.3 %copy-start.50 = (f32[4]{0:T(128)S(1)}, f32[4]{0:T(128)}, u32[]{:S(2)}) copy-start(f32[4]{0:T(128)} %get-tuple-element.331) | copy-start | bytes 52
  394.4 11.6 %copy-start.56 = (bf16[2048,1024]{1,0:T(8,128)(2,1)S(1)}, bf16[2048,1024]{1,0:T(8,128)(2,1)}, u32[]{:S(2)}) copy-start(bf16[2048,1024]{1,0:T(8,128)(2,1)} %all-gather.16.cloned.1.call-done) | copy-start | bytes 12582916
  406.0 4.6 copy-start.63
  406.0 4.6 copy-start.64
  406.0 4.6 copy-start.57
  416.7 60.5 %copy-start.21 = (f32[1024,256]{1,0:T(8,128)S(1)}, f32[1024,256]{1,0:T(8,128)}, u32[]{:S(2)}) copy-start(f32[1024,256]{1,0:T(8,128)} %wide_scatter.2) | copy-start | bytes 3145732
  416.7 60.5 %copy-start.44 = (f32[4]{0:T(128)S(1)}, f32[4]{0:T(128)}, u32[]{:S(2)}) copy-start(f32[4]{0:T(128)} %get-tuple-element.333) | copy-start | bytes 52
  416.7 60.5 %copy-start.46 = (f32[4]{0:T(128)S(1)}, f32[4]{0:T(128)}, u32[]{:S(2)}) copy-start(f32[4]{0:T(128)} %get-tuple-element.334) | copy-start | bytes 52
  526.0 6.3 copy-start.13
  534.7 4.4 copy-start.1
  541.6 6.3 copy-start.13
  550.3 4.3 copy-start.1
  562.5 7.6 copy-start.20
  562.5 202.5 %reduce-scatter.14.cloned.1.call-start = ((), (), s32[]{:S(2)}) async-start(), calls=%async_computation.17 | async-start | bytes 1310720 | tf_op jit(solution)/shard_map/reduce_scatter | solution.py:545
  567.1 199.7 %reduce-scatter.8.cloned.1.call-start = ((), (), s32[]{:S(2)}) async-start(), calls=%async_computation.14 | async-start | bytes 1310720 | tf_op jit(solution)/shard_map/reduce_scatter | solution.py:545
  576.1 192.6 %reduce-scatter.12.cloned.1.call-start = ((), (), s32[]{:S(2)}) async-start(), calls=%async_computation.16 | async-start | bytes 1310720 | tf_op jit(solution)/shard_map/reduce_scatter | solution.py:545
  582.1 188.3 %reduce-scatter.20.cloned.1.call-start = ((), (), s32[]{:S(2)}) async-start(), calls=%async_computation.20 | async-start | bytes 5242880 | tf_op jit(solution)/shard_map/reduce_scatter | solution.py:545
  591.6 181.7 %reduce-scatter.16.cloned.1.call-start = ((), (), s32[]{:S(2)}) async-start(), calls=%async_computation.18 | async-start | bytes 5242880 | tf_op jit(solution)/shard_map/reduce_scatter | solution.py:545
  601.5 209.6 %reduce-scatter.18.cloned.1.call-start = ((), (), s32[]{:S(2)}) async-start(), calls=%async_computation.19 | async-start | bytes 5242880 | tf_op jit(solution)/shard_map/reduce_scatter | solution.py:545
  611.0 6.6 copy-start.32
  611.0 6.6 copy-start.33
  611.0 7.7 copy-start.29
  617.5 5.7 copy-start.59
  618.7 4.6 copy-start.30
  623.2 4.5 copy-start.2
  623.2 4.6 copy-start.40
  627.8 7.9 copy-start.31
  644.9 69.3 %copy-start.48 = (f32[4]{0:T(128)S(1)}, f32[4]{0:T(128)}, u32[]{:S(2)}) copy-start(f32[4]{0:T(128)} %copy-done.47) | copy-start | bytes 52
  714.2 6.9 copy-start.52
  714.3 7.0 copy-start.51
  714.3 7.1 copy-start.49
  714.3 7.2 copy-start.41
  (21 other events, 61.5 us)
Sparse Core Ops, SparseCore 0:
  9.6 19.4 all-gather.9
  30.6 16.6 all-gather.7
  48.9 16.6 all-gather.11
  67.0 16.6 all-gather.13
  85.2 34.4 all-gather.15
  121.1 34.4 all-gather.17
  157.1 34.4 all-gather.19
  562.6 24.8 reduce-scatter.9
  590.0 24.7 reduce-scatter.13
  617.2 24.7 reduce-scatter.7
  644.6 24.7 reduce-scatter.11
  671.8 44.3 reduce-scatter.19
  718.8 45.0 reduce-scatter.15
  766.3 44.7 reduce-scatter.17

commit v2 on v1

v2 whole, which is shorter than its diff:
```python
import math
from functools import partial

import jax
import jax.numpy as jnp
from jax import lax
from jax.sharding import PartitionSpec as P
from jax.experimental import pallas as pl
from jax.experimental.pallas import tpu as pltpu

D = 2048
H = 16
CLIP_TAU = 6


EPSILON = 1e-05
MASKED = -1e30

BF = jnp.bfloat16
F32 = jnp.float32
NZ = 4
def place(count):
    w = lax.axis_index("wide")
    rows_y = count // NZ
    return w, w // rows_y, w % rows_y


def greet(w, count, spread=None):
    sem = pltpu.get_barrier_semaphore()
    for k in range(1, count):
        pl.semaphore_signal(sem, 1, device_id={"wide": (w + k) % count})
    more = spread.greet(sem) if spread else 0
    pl.semaphore_wait(sem, count - 1 + more)


def remote(src, dst, send, recv, target):
    return pltpu.make_async_remote_copy(src, dst, send, recv, device_id={"wide": target})


def dma(*shape):
    return pltpu.SemaphoreType.DMA(shape)


class Gather:
    def __init__(self, pos, count, chunks, x_ref, g_ref, sems):
        self.w, self.z, self.y = pos
        self.count, self.ny = count, count // NZ
        self.chunks, self.rows = chunks, g_ref.shape[0] // chunks
        self.x_ref, self.g_ref, self.bw = x_ref, g_ref, x_ref.shape[1]
        self.up_s, self.dn_s, self.y_s, self.z_r, self.y_r = sems

    @staticmethod
    def scratch(count, chunks):
        ny = count // NZ
        return [
            dma(NZ, chunks),
            dma(NZ, chunks),
            dma(NZ, ny - 1, chunks),
            dma(NZ, chunks),
            dma(NZ, ny - 1, chunks),
        ]

    def block(self, b, c):
        return self.g_ref.at[
            pl.ds(c * self.rows, self.rows), pl.ds(pl.multiple_of(b * self.bw, self.bw), self.bw)
        ]

    def source(self, b, c, own):
        if own:
            return self.x_ref.at[pl.ds(c * self.rows, self.rows)]
        return self.block(b, c)

    def up(self, s, zs, c):
        b = zs * self.ny + self.y
        target = (self.z + 1) * self.ny + self.y
        return remote(
            self.source(b, c, s == 0), self.block(b, c), self.up_s.at[s, c], self.z_r.at[zs, c], target
        )

    def down(self, s, zs, c):
        b = zs * self.ny + self.y
        target = (self.z - 1) * self.ny + self.y
        return remote(
            self.source(b, c, s == 0), self.block(b, c), self.dn_s.at[s, c], self.z_r.at[zs, c], target
        )

    def side(self, s, zs, k, c):
        b = zs * self.ny + self.y
        target = self.z * self.ny + (self.y + k) % self.ny
        return remote(
            self.source(b, c, s == 0),
            self.block(b, c),
            self.y_s.at[zs, k - 1, c],
            self.y_r.at[zs, k - 1, c],
            target,
        )

    def got(self, zs, c):
        b = zs * self.ny + self.y
        remote(self.block(b, c), self.block(b, c), self.up_s.at[0, c], self.z_r.at[zs, c], self.w).wait_recv()

    def got_side(self, zs):
        for k in range(1, self.ny):
            b = zs * self.ny + (self.y + self.ny - k) % self.ny
            for c in range(self.chunks):
                remote(
                    self.block(b, c),
                    self.block(b, c),
                    self.y_s.at[zs, k - 1, c],
                    self.y_r.at[zs, k - 1, c],
                    self.w,
                ).wait_recv()

    def begin(self, c):
        @pl.when(self.z < NZ - 1)
        def _():
            self.up(0, self.z, c).start()

        @pl.when(self.z > 0)
        def _():
            self.down(0, self.z, c).start()

        for k in range(1, self.ny):
            self.side(0, self.z, k, c).start()

    def place_own(self):
        self.g_ref[:, pl.ds(pl.multiple_of(self.w * self.bw, self.bw), self.bw)] = self.x_ref[...]

    def step(self, s):
        for c in range(self.chunks):

            @pl.when(self.z - s >= 0)
            def _():
                self.got(self.z - s, c)

                @pl.when(self.z < NZ - 1)
                def _():
                    self.up(s, self.z - s, c).start()

                for k in range(1, self.ny):
                    self.side(s, self.z - s, k, c).start()

            @pl.when(self.z + s < NZ)
            def _():
                self.got(self.z + s, c)

                @pl.when(self.z > 0)
                def _():
                    self.down(s, self.z + s, c).start()

                for k in range(1, self.ny):
                    self.side(s, self.z + s, k, c).start()

    def drain(self):
        for c in range(self.chunks):
            for s in range(NZ):

                @pl.when((self.z - s >= 0) & (self.z < NZ - 1))
                def _():
                    self.up(s, self.z - s, c).wait_send()

                @pl.when((self.z + s < NZ) & (self.z > 0))
                def _():
                    self.down(s, self.z + s, c).wait_send()

            for k in range(1, self.ny):
                self.side(0, self.z, k, c).wait_send()
            for s in range(1, NZ):
                for k in range(1, self.ny):

                    @pl.when(self.z - s >= 0)
                    def _():
                        self.side(s, self.z - s, k, c).wait_send()

                    @pl.when(self.z + s < NZ)
                    def _():
                        self.side(s, self.z + s, k, c).wait_send()

    def rest(self):
        for s in range(1, NZ):
            self.step(s)
        for zs in range(NZ):
            self.got_side(zs)


class Scatter:
    def __init__(self, pos, count, chunks, part, o_ref, scratch):
        self.w, self.z, self.y = pos
        self.count, self.ny = count, count // NZ
        self.chunks, self.rows = chunks, o_ref.shape[0] // chunks
        self.part, self.o_ref = part, o_ref
        (
            self.acc,
            self.ysnd,
            self.yrcv,
            self.usnd,
            self.urcv,
            self.dsnd,
            self.drcv,
            self.y_s,
            self.y_r,
            self.u_s,
            self.u_r,
            self.d_s,
            self.d_r,
        ) = scratch

    @staticmethod
    def scratch(count, chunks, tokens, bw):
        ny = count // NZ
        v = pltpu.VMEM
        rows = tokens // chunks
        return [
            v((rows, bw), F32),
            v((NZ, ny - 1, tokens, bw), BF),
            v((NZ, ny - 1, tokens, bw), BF),
            v((NZ, tokens, bw), BF),
            v((NZ, tokens, bw), BF),
            v((NZ, tokens, bw), BF),
            v((NZ, tokens, bw), BF),
            dma(NZ, ny - 1, chunks),
            dma(NZ, ny - 1, chunks),
            dma(NZ, chunks),
            dma(NZ, chunks),
            dma(NZ, chunks),
            dma(NZ, chunks),
        ]

    def order(self):
        half = self.z // (NZ // 2)
        plain = [3, 0, 2, 1]
        return [q + half * (NZ - 1 - 2 * q) for q in plain]

    def span(self, c):
        return pl.ds(pl.multiple_of(c * self.rows, self.rows), self.rows)

    def side(self, zd, k, c):
        rows = self.span(c)
        return remote(
            self.ysnd.at[zd, k - 1, rows],
            self.yrcv.at[zd, k - 1, rows],
            self.y_s.at[zd, k - 1, c],
            self.y_r.at[zd, k - 1, c],
            self.z * self.ny + (self.y + k) % self.ny,
        )

    def up(self, zd, c):
        rows = self.span(c)
        return remote(
            self.usnd.at[zd, rows],
            self.urcv.at[zd, rows],
            self.u_s.at[zd, c],
            self.u_r.at[zd, c],
            (self.z + 1) * self.ny + self.y,
        )

    def down(self, zd, c):
        rows = self.span(c)
        return remote(
            self.dsnd.at[zd, rows],
            self.drcv.at[zd, rows],
            self.d_s.at[zd, c],
            self.d_r.at[zd, c],
            (self.z - 1) * self.ny + self.y,
        )

    def begin(self, c):
        rows = self.span(c)
        for zd in self.order():
            for k in range(1, self.ny):
                block = zd * self.ny + (self.y + k) % self.ny
                self.ysnd[zd, k - 1, rows] = self.part(rows, block).astype(BF)
                self.side(zd, k, c).start()

    def relay(self, c):
        rows = self.span(c)
        for zd in self.order():
            value = self.part(rows, zd * self.ny + self.y)
            for k in range(1, self.ny):
                self.side(zd, k, c).wait_recv()
                value = value + self.yrcv[zd, k - 1, rows].astype(F32)
            self.acc[...] = value

            @pl.when(zd > self.z)
            def _():
                @pl.when(self.z > 0)
                def _():
                    self.up(zd, c).wait_recv()
                    self.acc[...] += self.urcv[zd, rows].astype(F32)

                self.usnd[zd, rows] = self.acc[...].astype(BF)
                self.up(zd, c).start()

            @pl.when(zd < self.z)
            def _():
                @pl.when(self.z < NZ - 1)
                def _():
                    self.down(zd, c).wait_recv()
                    self.acc[...] += self.drcv[zd, rows].astype(F32)

                self.dsnd[zd, rows] = self.acc[...].astype(BF)
                self.down(zd, c).start()

            @pl.when(zd == self.z)
            def _():
                self.o_ref[rows, :] = self.acc[...]

    def finish(self, c):
        rows = self.span(c)

        @pl.when(self.z > 0)
        def _():
            self.up(self.z, c).wait_recv()
            self.o_ref[rows, :] += self.urcv[self.z, rows].astype(F32)

        @pl.when(self.z < NZ - 1)
        def _():
            self.down(self.z, c).wait_recv()
            self.o_ref[rows, :] += self.drcv[self.z, rows].astype(F32)

    def drain(self):
        for c in range(self.chunks):
            for zd in range(NZ):
                for k in range(1, self.ny):
                    self.side(zd, k, c).wait_send()

                @pl.when(zd > self.z)
                def _():
                    self.up(zd, c).wait_send()

                @pl.when(zd < self.z)
                def _():
                    self.down(zd, c).wait_send()

    def run(self):
        self.begin(0)

        def body(c, carry):
            self.begin(c + 1)
            self.relay(c)
            return carry

        lax.fori_loop(0, self.chunks - 1, body, 0)
        self.relay(self.chunks - 1)
        for c in range(self.chunks):
            self.finish(c)


class Totals:
    def __init__(self, pos, count, own, buf, send, recv):
        self.w, self.count = pos[0], count
        self.own, self.buf, self.send, self.recv = own, buf, send, recv

    @staticmethod
    def scratch(count, tokens):
        return [
            pltpu.VMEM((8, tokens), F32),
            pltpu.VMEM((count, 8, tokens), F32),
            dma(count - 1),
            dma(count - 1),
        ]

    def copy(self, k):
        return remote(
            self.own, self.buf.at[k], self.send.at[k - 1], self.recv.at[k - 1], (self.w + k) % self.count
        )

    def exchange(self, first, second):
        rows = first.shape[0]
        lane = lax.broadcasted_iota(jnp.int32, (rows, 128), 1)
        pair = jnp.where(
            lane == 0, jnp.broadcast_to(first, (rows, 128)), jnp.broadcast_to(second, (rows, 128))
        )
        own = jnp.transpose(pair)[:8]
        self.own[...] = own
        for k in range(1, self.count):
            self.copy(k).start()
        total = own
        for k in range(1, self.count):
            self.copy(k).wait_recv()
            total = total + self.buf[k]
        for k in range(1, self.count):
            self.copy(k).wait_send()
        return total[0:1], total[1:2]


def column(row):
    return jnp.transpose(jnp.broadcast_to(row, (128, row.shape[1])))


class Spread:
    def __init__(self, groups, axes, shards, wholes, sems):
        self.d = lax.axis_index("dp")
        self.groups, self.chips = groups, groups // 2
        self.x, self.core = self.d // 2, self.d % 2
        self.axes, self.shards, self.wholes = axes, shards, wholes
        self.own_s, self.own_r, self.x_s, self.x_r, self.on_s, self.on_r = sems

    @staticmethod
    def scratch(groups, parts):
        chips = groups // 2
        return [
            dma(parts),
            dma(parts),
            dma(parts, chips - 1),
            dma(parts, chips - 1),
            dma(parts, chips - 1),
            dma(parts, chips - 1),
        ]

    def greet(self, sem):
        pl.semaphore_signal(sem, 1, device_id={"dp": self.x * 2 + 1 - self.core})
        for k in range(1, self.chips):
            pl.semaphore_signal(sem, 1, device_id={"dp": (self.x + k) % self.chips * 2 + self.core})
        return self.chips

    def place(self, n, d):
        shard, whole = self.shards[n], self.wholes[n]
        if self.axes[n] == 0:
            size = shard.shape[0]
            return whole.at[pl.ds(pl.multiple_of(d * size, size), size)]
        size = shard.shape[1]
        return whole.at[:, pl.ds(pl.multiple_of(d * size, size), size)]

    def copy(self, n, src, d, send, recv, target):
        return pltpu.make_async_remote_copy(src, self.place(n, d), send, recv, device_id={"dp": target})

    def other(self):
        return self.x * 2 + 1 - self.core

    def own(self, n):
        return self.copy(n, self.shards[n], self.d, self.own_s.at[n], self.own_r.at[n], self.other())

    def along(self, n, k):
        target = (self.x + k) % self.chips * 2 + self.core
        return self.copy(n, self.shards[n], self.d, self.x_s.at[n, k - 1], self.x_r.at[n, k - 1], target)

    def onward(self, n, k):
        origin = (self.x + self.chips - k) % self.chips * 2 + self.core
        return self.copy(
            n, self.place(n, origin), origin, self.on_s.at[n, k - 1], self.on_r.at[n, k - 1], self.other()
        )

    def begin(self, n):
        for k in range(1, self.chips):
            self.along(n, k).start()
        self.own(n).start()
        self.place(n, self.d)[...] = self.shards[n][...]

    def hand_over(self, n):
        for k in range(1, self.chips):
            origin = (self.x + self.chips - k) % self.chips * 2 + self.core
            self.copy(
                n, self.place(n, origin), origin, self.x_s.at[n, k - 1], self.x_r.at[n, k - 1], self.d
            ).wait_recv()
            self.onward(n, k).start()

    def finish(self, n):
        self.copy(n, self.shards[n], self.other(), self.own_s.at[n], self.own_r.at[n], self.d).wait_recv()
        for k in range(1, self.chips):
            origin = (self.x + self.chips - k) % self.chips * 2 + 1 - self.core
            self.copy(
                n, self.place(n, origin), origin, self.on_s.at[n, k - 1], self.on_r.at[n, k - 1], self.d
            ).wait_recv()
        self.own(n).wait_send()
        for k in range(1, self.chips):
            self.along(n, k).wait_send()
            self.onward(n, k).wait_send()


def tile_columns(block, bw):
    return jnp.concatenate([block] * (bw // 128), axis=1)


def rope_tables(length, head_size):
    half_size = head_size // 2
    inverse = 10000.0 ** (-2.0 * jnp.arange(half_size, dtype=jnp.float32) / head_size)
    angles = jnp.arange(length, dtype=jnp.float32)[:, None] * inverse[None, :]
    cosine_table = jnp.cos(angles)
    sine_table = jnp.sin(angles)
    return (
        jnp.concatenate([cosine_table, cosine_table], axis=1),
        jnp.concatenate([sine_table, sine_table], axis=1),
    )


def span_labels(positions, starts, lengths):
    inside = (positions[:, None] >= starts[None, :]) & (
        positions[:, None] < (starts + lengths)[None, :]
    )
    numbers = jnp.arange(1, starts.shape[0] + 1, dtype=jnp.int32)
    return jnp.sum(jnp.where(inside, numbers[None, :], 0), axis=1)


def hyper_rows(pre_grad, post_grad, mix_grad):
    return jnp.concatenate([pre_grad[:, None], post_grad[:, None], mix_grad], axis=1)


def block_columns(ref, rows, block, count):
    bw = ref.shape[1] // count
    return ref[rows, pl.ds(pl.multiple_of(block * bw, bw), bw)]


def block_rows(ref, block, count):
    bw = ref.shape[0] // count
    return ref[pl.ds(pl.multiple_of(block * bw, bw), bw), :]


def mm(left, right):
    return jnp.dot(left, right, preferred_element_type=F32)


def mm_t(left, right):
    return lax.dot_general(left, right, (((1,), (1,)), ((), ())), preferred_element_type=F32)


def t_mm(left, right):
    return lax.dot_general(left, right, (((0,), (0,)), ((), ())), preferred_element_type=F32)


def combine(values):
    total = values[0]
    for value in values[1:]:
        total = total + value
    return total


def joint(hyper_ref):
    return combine([hyper_ref[1, i, 0] * hyper_ref[0, i, 1] for i in range(4)])


def fold(product):
    rows, width = product.shape
    grouped = jnp.sum(product.reshape(rows // 8, 8, width), axis=0)
    return combine([grouped[:, k * 128 : (k + 1) * 128] for k in range(width // 128)])


def enter_kernel(hyper_ref, s_ref, c_ref, h1_ref, hs_ref, cd_ref, two_ref, sum_ref):
    s = [s_ref[k] for k in range(4)]
    c = [c_ref[k] for k in range(4)]
    h1_ref[...] = combine([hyper_ref[0, k, 0] * s[k] for k in range(4)])
    from_s = [combine([hyper_ref[1, i, 0] * hyper_ref[0, i, 2 + k] for i in range(4)]) for k in range(4)]
    hs_ref[...] = combine([from_s[k] * s[k] for k in range(4)])
    from_c = [combine([hyper_ref[0, i, 1] * hyper_ref[1, k, 2 + i] for i in range(4)]) for k in range(4)]
    cd_ref[...] = combine([from_c[k] * c[k] for k in range(4)])
    two_ref[...] = combine([hyper_ref[1, k, 1] * c[k] for k in range(4)]).astype(BF)

    @pl.when(pl.program_id(0) == 0)
    def _():
        sum_ref[...] = jnp.zeros_like(sum_ref)

    for i in range(4):
        for k in range(4):
            sum_ref[4 * i + k] += fold(c[i] * s[k])


def leave_kernel(hyper_ref, s_ref, c_ref, b1_ref, b2_ref, d2_ref, d1_ref, out_ref, grad_ref, sum_ref):
    s = [s_ref[k] for k in range(4)]
    c = [c_ref[k] for k in range(4)]
    b1, b2, d2, d1 = b1_ref[...], b2_ref[...], d2_ref[...], d1_ref[...]
    for i in range(4):
        coef = [combine([hyper_ref[1, i, 2 + j] * hyper_ref[0, j, 2 + k] for j in range(4)]) for k in range(4)]
        from_b = combine([hyper_ref[1, i, 2 + j] * hyper_ref[0, j, 1] for j in range(4)])
        out_ref[i] = combine([coef[k] * s[k] for k in range(4)]) + from_b * b1 + hyper_ref[1, i, 1] * b2
    for j in range(4):
        coef = [combine([hyper_ref[0, i, 2 + j] * hyper_ref[1, k, 2 + i] for i in range(4)]) for k in range(4)]
        from_d = combine([hyper_ref[0, i, 2 + j] * hyper_ref[1, i, 0] for i in range(4)])
        grad_ref[j] = combine([coef[k] * c[k] for k in range(4)]) + from_d * d2 + hyper_ref[0, j, 0] * d1

    @pl.when(pl.program_id(0) == 0)
    def _():
        sum_ref[...] = jnp.zeros_like(sum_ref)

    for k in range(4):
        sum_ref[k] += fold(c[k] * b1)
        sum_ref[4 + k] += fold(c[k] * b2)
        sum_ref[8 + k] += fold(d2 * s[k])
        sum_ref[12 + k] += fold(d1 * s[k])
    sum_ref[16] += fold(d2 * b1)


def total_kernel(count, groups, a_ref, b_ref, top_ref, o_ref, m_ref, own, dbuf, wbuf, mown, mbuf, ds, dr, ws, wr, ms, mr):
    w, d = lax.axis_index("wide"), lax.axis_index("dp")
    sem = pltpu.get_barrier_semaphore()
    for k in range(1, count):
        pl.semaphore_signal(sem, 1, device_id={"wide": (w + k) % count})
    for k in range(1, groups):
        pl.semaphore_signal(sem, 1, device_id={"dp": (d + k) % groups})
    pl.semaphore_wait(sem, count + groups - 2)
    na, nb = a_ref.shape[0], b_ref.shape[0]
    own[...] = jnp.zeros_like(own)
    for k in range(na):
        own[k : k + 1, :] = jnp.sum(a_ref[k], axis=0, keepdims=True)
    for k in range(nb):
        own[na + k : na + k + 1, :] = jnp.sum(b_ref[k], axis=0, keepdims=True)
    mown[...] = top_ref[...]

    def over_dp(src, dst, send, recv, k):
        return pltpu.make_async_remote_copy(
            src, dst.at[k - 1], send.at[k - 1], recv.at[k - 1], device_id={"dp": (d + k) % groups}
        )

    for k in range(1, groups):
        over_dp(own, dbuf, ds, dr, k).start()
        over_dp(mown, mbuf, ms, mr, k).start()
    total, best = own[...], mown[...]
    for k in range(1, groups):
        over_dp(own, dbuf, ds, dr, k).wait_recv()
        over_dp(mown, mbuf, ms, mr, k).wait_recv()
        total = total + dbuf[k - 1]
        best = jnp.maximum(best, mbuf[k - 1])
    m_ref[...] = best
    for k in range(1, groups):
        over_dp(own, dbuf, ds, dr, k).wait_send()
        over_dp(mown, mbuf, ms, mr, k).wait_send()
    own[...] = total

    def over_wide(k):
        return remote(own, wbuf.at[k - 1], ws.at[k - 1], wr.at[k - 1], (w + k) % count)

    for k in range(1, count):
        over_wide(k).start()
    for k in range(1, count):
        over_wide(k).wait_recv()
        total = total + wbuf[k - 1]
    for k in range(1, count):
        over_wide(k).wait_send()
    o_ref[...] = jnp.broadcast_to(jnp.sum(total, axis=1, keepdims=True), o_ref.shape)


def normalize(pos, count, hidden_ref, n_ref, i_ref, x_ref, totals):
    bw = hidden_ref.shape[1]
    width = count * bw
    hidden = hidden_ref[...]
    row_total, squares = totals.exchange(
        jnp.sum(hidden, axis=1, keepdims=True), jnp.sum(hidden * hidden, axis=1, keepdims=True)
    )
    centre = row_total / width
    inverse = lax.rsqrt(squares / width - centre * centre + EPSILON)
    inverse_cols = column(inverse)
    i_ref[...] = inverse_cols
    normed = (hidden_ref[...] - tile_columns(column(centre), bw)) * tile_columns(inverse_cols, bw)
    n_ref[...] = normed
    x_ref[...] = normed.astype(BF)


def denormalize(pos, count, sum_ref, n_ref, i_ref, o_ref, totals):
    bw = n_ref.shape[1]
    width = count * bw
    grads = sum_ref[...]
    row_total, cross = totals.exchange(
        jnp.sum(grads, axis=1, keepdims=True), jnp.sum(grads * n_ref[...], axis=1, keepdims=True)
    )
    o_ref[...] = tile_columns(i_ref[...], bw) * (
        sum_ref[...]
        - tile_columns(column(row_total / width), bw)
        - n_ref[...] * tile_columns(column(cross / width), bw)
    )


def first_kernel(count, groups, chunks, h_ref, sq, sk, sv, so, g_ref, n_ref, i_ref, wq, wk, wv, wo, x_ref, *rest):
    pos = place(count)
    spread = Spread(groups, (0, 0, 0, 1), (sq, sk, sv, so), (wq, wk, wv, wo), rest[:6])
    greet(pos[0], count, spread)
    for n in range(4):
        spread.begin(n)
    totals = Totals(pos, count, *rest[6:10])
    normalize(pos, count, h_ref, n_ref, i_ref, x_ref, totals)
    gather = Gather(pos, count, chunks, x_ref, g_ref, rest[10:])
    for c in range(chunks):
        gather.begin(c)
    gather.place_own()
    for n in range(2):
        spread.hand_over(n)
    gather.step(1)
    for n in range(2, 4):
        spread.hand_over(n)
    gather.step(2)
    gather.step(3)
    for zs in range(NZ):
        gather.got_side(zs)
    for n in range(4):
        spread.finish(n)
    gather.drain()


def head_mask(doc_rows, doc_cols, lab_rows, lab_cols, r0, c0, rows, cols):
    q = r0 + lax.broadcasted_iota(jnp.int32, (rows, cols), 0)
    k = c0 + lax.broadcasted_iota(jnp.int32, (rows, cols), 1)
    same = doc_rows == doc_cols
    joined = (lab_rows > 0) & (lab_rows == lab_cols)
    return same & ((k <= q) | joined)


QB = 256
DOC_MAX = 512
SPANS = 2


def key_range(r0, length):
    low = max(0, (r0 - DOC_MAX + 1) // QB * QB)
    region = length // SPANS
    high = min(length, (r0 // region + 1) * region)
    return low, high


def turn(values, cos, sin):
    half = values.shape[1] // 2
    turned = jnp.concatenate([-values[:, half:], values[:, :half]], axis=1)
    return values * cos + turned * sin


def turn_back(grads, cos, sin):
    half = grads.shape[1] // 2
    scaled = grads * sin
    turned = jnp.concatenate([scaled[:, half:], -scaled[:, :half]], axis=1)
    return grads * cos + turned


HD = D // H


def attention_rows(h, r0, scale, length, q_ref, k_ref, v_ref, o_ref, lse_ref, top_ref, masks):
    cols = slice(h * HD, (h + 1) * HD)
    low, high = key_range(r0, length)
    doc_c, doc_r, lab_c, lab_r = masks
    s = mm_t(q_ref[r0 : r0 + QB, cols], k_ref[low:high, cols]) * scale
    allowed = head_mask(
        doc_c[r0 : r0 + QB, :1],
        doc_r[:1, low:high],
        lab_c[r0 : r0 + QB, :1],
        lab_r[:1, low:high],
        r0,
        low,
        QB,
        high - low,
    )
    s = jnp.where(allowed, s, MASKED)
    largest = jnp.max(s, axis=1, keepdims=True)
    e = jnp.exp(s - largest)
    total = jnp.sum(e, axis=1, keepdims=True)
    weights = (e / total).astype(BF)
    o_ref[r0 : r0 + QB, cols] = mm(weights, v_ref[low:high, cols]).astype(BF)
    lse_ref[h, r0 : r0 + QB, :] = jnp.broadcast_to(largest + jnp.log(total), (QB, 128))
    top_ref[h : h + 1, :] = jnp.maximum(top_ref[h : h + 1, :], jnp.max(largest))


def attention_kernel(count, chunks, scale, x_ref, wq, wk, wv, cos_ref, sin_ref, doc_c, doc_r, lab_c, lab_r, two_ref,
                     q_ref, k_ref, v_ref, o_ref, lse_ref, top_ref, g_ref, *sems):
    pos = place(count)
    greet(pos[0], count)
    gather = Gather(pos, count, chunks, two_ref, g_ref, sems)
    for c in range(chunks):
        gather.begin(c)
    gather.place_own()
    length, width = q_ref.shape
    heads = width // HD
    top_ref[...] = jnp.full(top_ref.shape, MASKED, F32)
    v_ref[...] = mm(x_ref[...], wv[...]).astype(BF)
    for target, weight in ((q_ref, wq), (k_ref, wk)):
        for h in range(heads):
            cols = slice(h * HD, (h + 1) * HD)
            raw = mm(x_ref[...], weight[:, cols])
            target[:, cols] = turn(raw, cos_ref[...], sin_ref[...]).astype(BF)
    gather.step(1)
    masks = (doc_c, doc_r, lab_c, lab_r)
    todo = [(h, r0) for h in range(heads) for r0 in range(0, length, QB)]
    for n, (h, r0) in enumerate(todo):
        attention_rows(h, r0, scale, length, q_ref, k_ref, v_ref, o_ref, lse_ref, top_ref, masks)
        if n == len(todo) // 2 - 1:
            gather.step(2)
    gather.step(3)
    for zs in range(NZ):
        gather.got_side(zs)
    gather.drain()


def middle_kernel(count, g_chunks, s_chunks, hyper_ref, att_ref, wo_ref, hs_ref, wg_hbm, wu_hbm, wd_hbm, two_hbm,
                  b1_ref, n_ref, i_ref, x2_ref, hid_ref, dg_ref, du_ref,
                  wg, wu, wd, two, load, dhid, h_ref, x_ref, *rest):
    pos = place(count)
    loads = [
        pltpu.make_async_copy(src, dst, load.at[n])
        for n, (src, dst) in enumerate(((wd_hbm, wd), (two_hbm, two), (wg_hbm, wg), (wu_hbm, wu)))
    ]
    for copy in loads:
        copy.start()
    greet(pos[0], count)

    def part(rows, block):
        return mm(att_ref[rows, :], block_columns(wo_ref, slice(None), block, count))

    scatter = Scatter(pos, count, s_chunks, part, b1_ref, rest[:13])
    scatter.run()
    h_ref[...] = hs_ref[...] + joint(hyper_ref) * b1_ref[...]
    totals = Totals(pos, count, *rest[13:17])
    normalize(pos, count, h_ref, n_ref, i_ref, x_ref, totals)
    gather = Gather(pos, count, g_chunks, x_ref, x2_ref, rest[17:])
    for c in range(g_chunks):
        gather.begin(c)
    gather.place_own()
    tokens, width = hid_ref.shape
    tile = 256
    half = tokens // 2
    steps = width // tile

    def where(n):
        rows = pl.ds(pl.multiple_of((n // steps) * half, half), half)
        cols = pl.ds(pl.multiple_of((n % steps) * tile, tile), tile)
        return rows, cols

    def down_back(n, carry):
        rows, cols = where(n)
        dhid[rows, cols] = mm_t(two[rows, :], wd[cols, :])
        return carry

    loads[0].wait()
    loads[1].wait()
    gather.step(1)
    lax.fori_loop(0, steps, down_back, 0)
    gather.step(2)
    lax.fori_loop(steps, 2 * steps, down_back, 0)
    gather.step(3)
    for zs in range(NZ):
        gather.got_side(zs)
    loads[2].wait()
    loads[3].wait()

    def feed(n, carry):
        rows, cols = where(n)
        gate = mm(x2_ref[rows, :], wg[:, cols])
        up = mm(x2_ref[rows, :], wu[:, cols])
        sg = 1.0 / (1.0 + jnp.exp(-gate))
        back = dhid[rows, cols]
        swish = gate * sg
        hid_ref[rows, cols] = (swish * up).astype(BF)
        dg_ref[rows, cols] = (back * up * sg * (1.0 + gate * (1.0 - sg))).astype(BF)
        du_ref[rows, cols] = (back * swish).astype(BF)
        return carry

    lax.fori_loop(0, 2 * steps, feed, 0)
    scatter.drain()
    gather.drain()


def second_kernel(count, g_chunks, s_chunks, hyper_ref, dg_ref, du_ref, wg, wu, n_ref, i_ref, cd_ref,
                  d2_ref, one_ref, sum_ref, x_ref, *rest):
    pos = place(count)
    greet(pos[0], count)

    def part(rows, block):
        return mm_t(dg_ref[rows, :], block_rows(wg, block, count)) + mm_t(
            du_ref[rows, :], block_rows(wu, block, count)
        )

    scatter = Scatter(pos, count, s_chunks, part, sum_ref, rest[:13])
    scatter.run()
    totals = Totals(pos, count, *rest[13:17])
    denormalize(pos, count, sum_ref, n_ref, i_ref, d2_ref, totals)
    x_ref[...] = (cd_ref[...] + joint(hyper_ref) * d2_ref[...]).astype(BF)
    gather = Gather(pos, count, g_chunks, x_ref, one_ref, rest[17:])
    for c in range(g_chunks):
        gather.begin(c)
    gather.place_own()
    gather.rest()
    scatter.drain()
    gather.drain()


def back_rows(h, r0, scale, length, q_ref, k_ref, v_ref, do_ref, lse_ref, dq_acc, dk_acc, dv_acc, masks):
    cols = slice(h * HD, (h + 1) * HD)
    rows = slice(r0, r0 + QB)
    low, high = key_range(r0, length)
    doc_c, doc_r, lab_c, lab_r = masks
    q, k, v, do = q_ref[rows, cols], k_ref[low:high, cols], v_ref[low:high, cols], do_ref[rows, cols]
    s = mm_t(q, k) * scale
    allowed = head_mask(
        doc_c[rows, :1], doc_r[:1, low:high], lab_c[rows, :1], lab_r[:1, low:high], r0, low, QB, high - low
    )
    weights = jnp.where(allowed, jnp.exp(jnp.where(allowed, s, MASKED) - lse_ref[h, rows, :1]), 0.0)
    grad = mm_t(do, v)
    centre = jnp.sum(weights * grad, axis=1, keepdims=True)
    ds = (weights * (grad - centre)).astype(BF)
    dq_acc[rows, cols] = mm(ds, k) * scale
    dk_acc[low:high, cols] += t_mm(ds, q)
    dv_acc[low:high, cols] += t_mm(weights.astype(BF), do)


def attention_back_kernel(count, s_chunks, scale, one_ref, wo_ref, q_ref, k_ref, v_ref, lse_ref, cos_ref, sin_ref,
                          doc_c, doc_r, lab_c, lab_r, hid_ref, wd_ref,
                          dq_ref, dk_ref, dv_ref, b2_ref, do_ref, dq_acc, dk_acc, dv_acc, *scratch):
    pos = place(count)
    greet(pos[0], count)

    def part(rows, block):
        return mm(hid_ref[rows, :], block_columns(wd_ref, slice(None), block, count))

    scatter = Scatter(pos, count, s_chunks, part, b2_ref, scratch)
    scatter.begin(0)
    length, width = q_ref.shape
    heads = width // HD
    do_ref[...] = mm_t(one_ref[...], wo_ref[...]).astype(BF)
    dk_acc[...] = jnp.zeros_like(dk_acc)
    dv_acc[...] = jnp.zeros_like(dv_acc)
    masks = (doc_c, doc_r, lab_c, lab_r)
    todo = [(h, r0) for h in range(heads) for r0 in range(0, length, QB)]
    for n, (h, r0) in enumerate(todo):
        if n * s_chunks % len(todo) == 0 or s_chunks > len(todo):
            c = n * s_chunks // len(todo)
            if c + 1 < s_chunks:
                scatter.begin(c + 1)
            scatter.relay(c)
        back_rows(h, r0, scale, length, q_ref, k_ref, v_ref, do_ref, lse_ref, dq_acc, dk_acc, dv_acc, masks)
    for h in range(heads):
        cols = slice(h * HD, (h + 1) * HD)
        dq_ref[:, cols] = turn_back(dq_acc[:, cols], cos_ref[...], sin_ref[...]).astype(BF)
        dk_ref[:, cols] = turn_back(dk_acc[:, cols] * scale, cos_ref[...], sin_ref[...]).astype(BF)
    dv_ref[...] = dv_acc[...].astype(BF)
    for c in range(s_chunks):
        scatter.finish(c)
    scatter.drain()


def last_kernel(count, s_chunks, dq_ref, dk_ref, dv_ref, wq, wk, wv, n_ref, i_ref, d1_ref, sum_ref, *rest):
    pos = place(count)
    greet(pos[0], count)

    def part(rows, block):
        return (
            mm_t(dq_ref[rows, :], block_rows(wq, block, count))
            + mm_t(dk_ref[rows, :], block_rows(wk, block, count))
            + mm_t(dv_ref[rows, :], block_rows(wv, block, count))
        )

    scatter = Scatter(pos, count, s_chunks, part, sum_ref, rest[:13])
    scatter.run()
    totals = Totals(pos, count, *rest[13:])
    denormalize(pos, count, sum_ref, n_ref, i_ref, d1_ref, totals)
    scatter.drain()


VM = pl.BlockSpec(memory_space=pltpu.VMEM)
SM = pl.BlockSpec(memory_space=pltpu.SMEM)
ANY = pl.BlockSpec(memory_space=pl.ANY)


def call(kernel, ident, outs, ins, scratch, name, specs=None):
    return pl.pallas_call(
        kernel,
        out_shape=outs,
        in_specs=specs or [VM] * len(ins),
        out_specs=tuple(VM for _ in outs) if isinstance(outs, tuple) else VM,
        scratch_shapes=scratch,
        compiler_params=pltpu.CompilerParams(
            collective_id=ident, has_side_effects=True, vmem_limit_bytes=63 * 1024 * 1024
        ),
        name=name,
        cost_estimate=pl.CostEstimate(flops=50_000_000_000, bytes_accessed=8_000_000, transcendentals=0),
    )(*ins)


def shape(dtype, *dims):
    return jax.ShapeDtypeStruct(dims, dtype)


AG_CHUNKS = 8
RS_CHUNKS = 4
ROWS = 128


def rows_call(kernel, hyper, ins, outs, name):
    tokens = ins[0].shape[-2]

    def spec(a):
        if a.shape[-2] != tokens:
            return pl.BlockSpec(a.shape, lambda t: (0,) * len(a.shape))
        if len(a.shape) == 3:
            return pl.BlockSpec((a.shape[0], ROWS, a.shape[2]), lambda t: (0, t, 0))
        return pl.BlockSpec((ROWS, a.shape[1]), lambda t: (t, 0))

    return pl.pallas_call(
        kernel,
        grid=(tokens // ROWS,),
        out_shape=outs,
        in_specs=[SM] + [spec(a) for a in ins],
        out_specs=tuple(spec(a) for a in outs),
        compiler_params=pltpu.CompilerParams(vmem_limit_bytes=32 * 1024 * 1024),
        name=name,
        cost_estimate=pl.CostEstimate(flops=1_000_000_000, bytes_accessed=20_000_000, transcendentals=0),
    )(hyper, *ins)


def weight_sum(left, right):
    return lax.dot_general(left, right, (((0,), (0,)), ((), ())), preferred_element_type=F32).astype(BF)


def weight_shard(value, axis):
    return lax.psum_scatter(value, "dp", scatter_dimension=axis, tiled=True).astype(F32)


def hyper_grad(hyper, v):
    pre1, post0, mix0, mix1 = hyper[1, :, 0], hyper[0, :, 1], hyper[0, :, 2:], hyper[1, :, 2:]
    cs, cb1, cb2, d2s, d1s, d2b1 = v[:16].reshape(4, 4), v[16:20], v[20:24], v[24:28], v[28:32], v[32]
    flat = partial(jnp.sum, axis=-1)
    g1_pre = flat(mix0 * d2s[None, :]) + post0 * d2b1
    g1_mix = jnp.sum(cs[:, None, :] * mix0[None, :, :], axis=2) + cb1[:, None] * post0[None, :]
    g0_post = jnp.sum(mix1 * cb1[:, None], axis=0) + pre1 * d2b1
    g0_mix = jnp.sum(mix1[:, :, None] * cs[:, None, :], axis=0) + pre1[:, None] * d2s[None, :]
    return jnp.stack([hyper_rows(d1s, g0_post, g0_mix), hyper_rows(g1_pre, cb2, g1_mix)])


def per_device(
    streams,
    cotangent,
    w_query,
    w_key,
    w_value,
    w_out,
    w_gate,
    w_up,
    w_down,
    hyper,
    doc_ids,
    span_starts,
    span_lengths,
):
    length = doc_ids.shape[1]
    tokens, bw = streams.shape[1:]
    count, groups = lax.axis_size("wide"), lax.axis_size("dp")
    heads = bw // HD
    scale = 1.0 / math.sqrt(HD)
    cos, sin = rope_tables(length, HD)
    labels = span_labels(jnp.arange(length, dtype=jnp.int32), span_starts[0], span_lengths[0])
    doc_r = jnp.broadcast_to(doc_ids, (8, length))
    lab_r = jnp.broadcast_to(labels[None, :], (8, length))
    doc_c = jnp.broadcast_to(doc_ids[0][:, None], (length, 128))
    lab_c = jnp.broadcast_to(labels[:, None], (length, 128))
    masks = [doc_c, doc_r, lab_c, lab_r]
    gate_w, up_w, down_w = (
        lax.all_gather(w_gate, "dp", axis=0, tiled=True),
        lax.all_gather(w_up, "dp", axis=0, tiled=True),
        lax.all_gather(w_down, "dp", axis=1, tiled=True),
    )
    hidden_units = gate_w.shape[1]
    small = shape(F32, tokens, bw)
    low = shape(BF, tokens, bw)
    whole = shape(BF, tokens, count * bw)
    stat = shape(F32, tokens, 128)
    wide_low = shape(BF, tokens, hidden_units)
    v = pltpu.VMEM
    scatter_scratch = Scatter.scratch(count, RS_CHUNKS, tokens, bw)
    gather_scratch = Gather.scratch(count, AG_CHUNKS)
    total_scratch = Totals.scratch(count, tokens)

    h_one, h_streams, cot_one, two_part, sums_a = rows_call(
        enter_kernel, hyper, [streams, cotangent], (small, small, small, low, shape(F32, 16, 8, 128)), "enter"
    )
    tall = shape(BF, count * bw, bw)
    x_one, kept_one, inverse_one, query_w, key_w, value_w, out_w = call(
        partial(first_kernel, count, groups, AG_CHUNKS),
        0,
        (whole, small, stat, tall, tall, tall, shape(BF, bw, count * bw)),
        [h_one, w_query, w_key, w_value, w_out],
        [v((tokens, bw), BF)] + Spread.scratch(groups, 4) + total_scratch + gather_scratch,
        "first",
    )
    queries, keys, values, attended, log_sums, tops, two_grad = call(
        partial(attention_kernel, count, AG_CHUNKS, scale),
        1,
        (low, low, low, low, shape(F32, heads, tokens, 128), shape(F32, 8, 128), whole),
        [x_one, query_w, key_w, value_w, cos, sin] + masks + [two_part],
        gather_scratch,
        "attention",
    )
    branch_one, kept_two, inverse_two, x_two, hidden, gate_grad, up_grad = call(
        partial(middle_kernel, count, AG_CHUNKS, RS_CHUNKS),
        2,
        (small, small, stat, whole, wide_low, wide_low, wide_low),
        [hyper, attended, out_w, h_streams, gate_w, up_w, down_w, two_grad],
        [
            v(gate_w.shape, BF),
            v(up_w.shape, BF),
            v(down_w.shape, BF),
            v((tokens, count * bw), BF),
            dma(4),
            v((tokens, hidden_units), F32),
            v((tokens, bw), F32),
            v((tokens, bw), BF),
        ]
        + scatter_scratch
        + total_scratch
        + gather_scratch,
        "middle",
        [SM, VM, VM, VM, ANY, ANY, ANY, ANY],
    )
    down_sum, gate_sum, up_sum = (
        weight_sum(hidden, two_grad),
        weight_sum(x_two, gate_grad),
        weight_sum(x_two, up_grad),
    )
    gate_grad, up_grad, hidden, down_sum, gate_sum, up_sum = lax.optimization_barrier(
        (gate_grad, up_grad, hidden, down_sum, gate_sum, up_sum)
    )
    down_shard, gate_shard, up_shard = (
        weight_shard(down_sum, 1),
        weight_shard(gate_sum, 0),
        weight_shard(up_sum, 0),
    )
    h_two_grad, one_grad = call(
        partial(second_kernel, count, AG_CHUNKS, RS_CHUNKS),
        3,
        (small, whole),
        [hyper, gate_grad, up_grad, gate_w, up_w, kept_two, inverse_two, cot_one],
        [v((tokens, bw), F32), v((tokens, bw), BF)] + scatter_scratch + total_scratch + gather_scratch,
        "second",
        [SM] + [VM] * 7,
    )
    query_low, key_low, value_low, branch_two = call(
        partial(attention_back_kernel, count, RS_CHUNKS, scale),
        4,
        (low, low, low, small),
        [one_grad, out_w, queries, keys, values, log_sums, cos, sin] + masks + [hidden, down_w],
        [v((tokens, bw), BF)] + [v((tokens, bw), F32)] * 3 + scatter_scratch,
        "attention_back",
    )
    query_low, key_low, value_low, one_grad, down_shard, gate_shard, up_shard = lax.optimization_barrier(
        (query_low, key_low, value_low, one_grad, down_shard, gate_shard, up_shard)
    )
    query_low, key_low, value_low, out_sum, query_sum, key_sum, value_sum = lax.optimization_barrier(
        (
            query_low,
            key_low,
            value_low,
            weight_sum(attended, one_grad),
            weight_sum(x_one, query_low),
            weight_sum(x_one, key_low),
            weight_sum(x_one, value_low),
        )
    )
    out_shard, query_shard, key_shard, value_shard = (
        weight_shard(out_sum, 1),
        weight_shard(query_sum, 0),
        weight_shard(key_sum, 0),
        weight_shard(value_sum, 0),
    )
    h_one_grad = call(
        partial(last_kernel, count, RS_CHUNKS),
        5,
        small,
        [query_low, key_low, value_low, query_w, key_w, value_w, kept_one, inverse_one],
        [v((tokens, bw), F32)] + scatter_scratch + total_scratch,
        "last",
    )
    streams_shape = shape(F32, 4, tokens, bw)
    out_streams, streams_grad, sums_b = rows_call(
        leave_kernel,
        hyper,
        [streams, cotangent, branch_one, branch_two, h_two_grad, h_one_grad],
        (streams_shape, streams_shape, shape(F32, 17, 8, 128)),
        "leave",
    )
    sums, best = call(
        partial(total_kernel, count, groups),
        6,
        (shape(F32, 40, 128), shape(F32, 8, 128)),
        [sums_a, sums_b, tops],
        [
            v((40, 128), F32),
            v((groups - 1, 40, 128), F32),
            v((count - 1, 40, 128), F32),
            v((8, 128), F32),
            v((groups - 1, 8, 128), F32),
            dma(groups - 1),
            dma(groups - 1),
            dma(count - 1),
            dma(count - 1),
            dma(groups - 1),
            dma(groups - 1),
        ],
        "totals",
    )
    head_top = best[:heads, 0]
    clip_scale = jnp.sqrt(CLIP_TAU / jnp.maximum(head_top, CLIP_TAU))
    columns = jnp.repeat(clip_scale, HD)[None, :]
    return (
        out_streams,
        streams_grad,
        query_shard,
        key_shard,
        value_shard,
        out_shard,
        gate_shard,
        up_shard,
        down_shard,
        hyper_grad(hyper, sums[:, 0]),
        clip_scale,
        w_query.astype(F32) * columns,
        w_key.astype(F32) * columns,
    )


def solution(mesh):
    return jax.shard_map(
        per_device,
        mesh=mesh,
        in_specs=(
            P(None, "dp", "wide"),
            P(None, "dp", "wide"),
            P("dp", "wide"),
            P("dp", "wide"),
            P("dp", "wide"),
            P("wide", "dp"),
            P("dp", "wide"),
            P("dp", "wide"),
            P("wide", "dp"),
            P(),
            P("dp", None),
            P("dp", None),
            P("dp", None),
        ),
        out_specs=(
            P(None, "dp", "wide"),
            P(None, "dp", "wide"),
            P("dp", "wide"),
            P("dp", "wide"),
            P("dp", "wide"),
            P("wide", "dp"),
            P("dp", "wide"),
            P("dp", "wide"),
            P("wide", "dp"),
            P(),
            P("wide"),
            P("dp", "wide"),
            P("dp", "wide"),
        ),
        check_vma=False,
    )
```

time: 825 us -> 630 us (0.76)
  matrix products: 161 us -> 45.9 us
  other arithmetic: 89 us -> 22.5 us
  Pallas kernels: 447 us -> 496 us
  blocking collectives: 47.5 us -> 0 us
  waiting for transfers between devices: 39.4 us -> 15.3 us
  local copies, waits for them, and re-layouts: 17.3 us -> 26.2 us
    dot_general x35 -> x7, matrix products: 161 us -> 45.9 us  [weight_sum(): lax.dot_general(left, right, (((0,), (0,)), ((), ())), preferred_element_...]
    reduce_sum x8 -> x2, other arithmetic: 54.7 us -> 0.28 us  [the longest x1 0.19 us: hyper_grad(): g0_post = jnp.sum(mix1 * cb1[:, None], axis=0) + pre1 * d2b1]
    pallas_call x8 -> x9, Pallas kernels: 447 us -> 496 us  [the longest x7 484 us: call(): pl.pallas_call(kernel, out_shape=outs, in_specs=specs or [VM] * len(ins),...]
    psum x1 -> x0, blocking collectives: 41.7 us -> none  [per_device(): lax.psum(jnp.stack([hyper_rows(attn_pre_grad, attn_post_grad, attn_mix_gr...]
    reduce_scatter x7, waiting for transfers between devices: 34.9 us -> 10.4 us  [weight_shard(): lax.psum_scatter(value, 'dp', scatter_dimension=axis, tiled=True)]
    unnamed x118 -> x54, local copies, waits for them, and re-layouts: 2.43 us -> 19.5 us
    convert_element_type x13 -> x7, other arithmetic: 19 us -> 15.6 us  [weight_shard(): lax.psum_scatter(value, 'dp', scatter_dimension=axis, tiled=True)]
  transfers between devices with their start and end apart: 14 -> 10, of which waited for: 1 -> 1; matrix products, arithmetic and copies ran while one was open for 22% -> 4% of each run, Pallas kernels for 30% -> 60%
where the time goes in v2:
time: 630 us; the launch traced here: 621 us
  Pallas kernels  496 us (79%)
  matrix products  45.9 us (7%)
  local copies, waits for them, and re-layouts  26.2 us (4%)
  other arithmetic  22.5 us (4%)
  waiting for transfers between devices  15.3 us (2%)
  between operations  14.9 us (2%)
    pallas_call x7, Pallas kernels, call(): pl.pallas_call(kernel, out_shape=outs, in_specs=specs or [VM] * len(ins),...  484 us
    dot_general x7, matrix products, weight_sum(): lax.dot_general(left, right, (((0,), (0,)), ((), ())), preferred_element_...  45.9 us
    unnamed x54, local copies, waits for them, and re-layouts  19.5 us
    convert_element_type x7, other arithmetic, weight_shard(): lax.psum_scatter(value, 'dp', scatter_dimension=axis, tiled=True)  15.6 us
  transfers between devices with their start and end apart: 10, of which 1 were waited for; matrix products, arithmetic and copies ran while one was open for 4% of the time, Pallas kernels for 60%

profile of v2, /device:TPU:0, one launch (start us, length us, event | category | flops | bytes accessed | tf_op | source)
XLA Modules:
  0.0 621.1 jit_solution(633258174200460926)
XLA Ops:
  7.2 0.7 all-gather.4.cloned.1.call-update
  8.0 0.7 all-gather.6.cloned.1.call-update
  8.7 0.7 all-gather.8.cloned.1.call-update
  9.5 2.2 copy-done
  11.6 2.2 copy-done.2
  13.8 0.7 copy-done.8
  14.5 3.9 enter.1
  18.5 1.0 copy-done.10
  19.4 1.0 copy-done.11
  20.4 1.0 copy-done.12
  21.4 0.8 copy-done.13
  22.2 0.6 copy-done.15
  22.8 75.1 %first.1 = (bf16[1024,2048]{1,0:T(8,128)(2,1)}, f32[1024,256]{1,0:T(8,128)}, f32[1024,128]{1,0:T(8,128)}, bf16[2048,256]{1,0:T(8,128)(2,1)}, bf16[2048,256]{1,0:...) custom-call(f32[1024,256]{1,0:T(8,128)} %copy-done.12, bf16[512,256]{1,0:T(8,128)(2,1)} %sq.1, ...), custom_call_target="tpu_custom_call" | custom-call | flops 49999998976 | bytes 8000000 | tf_op jit(solution)/shard_map/first/pallas_call | solution.py:948
  98.1 1.9 fusion
  100.0 1.3 pad_maximum_fusion
  101.4 1.0 broadcast_in_dim.25.doc_c
  102.3 0.6 broadcast_in_dim.26.doc_r
  103.0 1.0 broadcast_in_dim.29.lab_c
  104.0 0.6 broadcast_in_dim.30.lab_r
  104.6 58.5 %attention.1 = (bf16[1024,256]{1,0:T(8,128)(2,1)}, bf16[1024,256]{1,0:T(8,128)(2,1)}, bf16[1024,256]{1,0:T(8,128)(2,1)}, bf16[1024,256]{1,0:T(8,128)(2,1)}, f32[...) custom-call(bf16[1024,2048]{1,0:T(8,128)(2,1)} %get-tuple-element.71.x_ref, ...), custom_call_target="tpu_custom_call" | custom-call | flops 49999998976 | bytes 8000000 | tf_op jit(solution)/shard_map/attention/pallas_call | solution.py:948
  163.2 124.3 %middle.1 = (f32[1024,256]{1,0:T(8,128)}, f32[1024,256]{1,0:T(8,128)}, f32[1024,128]{1,0:T(8,128)}, bf16[1024,2048]{1,0:T(8,128)(2,1)}, bf16[1024,1024]{1,0:T(8,...) custom-call(f32[2,4,6]{2,1,0:T(4,128)} %hyper_ref.7, bf16[1024,256]{1,0:T(8,128)(2,1)} %get-tuple-element.76.att_ref, ...), custom_call_target="tpu_custom_call" | custom-call | flops 49999998976 | bytes 8000000 | tf_op jit(solution)/shard_map/middle/pallas_call | solution.py:948
  287.5 9.5 %convolution_convert_fusion.2 = bf16[1024,2048]{1,0:T(8,128)(2,1)} fusion(bf16[1024,1024]{1,0:T(8,128)(2,1)} %get-tuple-element.95.hid_ref, bf16[1024,2048]{1,0:T(8,128)(2,1)} %get-tuple-element.79.two_hbm), kind=kOutput, calls=%fused_computation.2 | convolution fusion | flops 4297064448 | bytes 10485760 | tf_op jit(solution)/shard_map/dot_general | solution.py:994
  297.0 8.7 %convolution_convert_fusion.1 = bf16[2048,1024]{1,0:T(8,128)(2,1)} fusion(bf16[1024,2048]{1,0:T(8,128)(2,1)} %get-tuple-element.84, bf16[1024,1024]{1,0:T(8,128)(2,1)S(1)} %copy-done.26), kind=kOutput, calls=%fused_computation.1 | convolution fusion | flops 4297064448 | bytes 10485760 | tf_op jit(solution)/shard_map/dot_general | solution.py:994
  305.7 9.5 %convolution_convert_fusion = bf16[2048,1024]{1,0:T(8,128)(2,1)} fusion(bf16[1024,2048]{1,0:T(8,128)(2,1)} %get-tuple-element.84, bf16[1024,1024]{1,0:T(8,128)(2,1)} %get-tuple-element.86.du_ref), kind=kOutput, calls=%fused_computation | convolution fusion | flops 4297064448 | bytes 10485760 | tf_op jit(solution)/shard_map/dot_general | solution.py:994
  315.2 0.5 reduce-scatter.10.cloned.1.call-update
  315.8 0.5 reduce-scatter.12.cloned.1.call-update
  316.4 106.9 %second.1 = (f32[1024,256]{1,0:T(8,128)}, bf16[1024,2048]{1,0:T(8,128)(2,1)}) custom-call(f32[2,4,6]{2,1,0:T(4,128)} %hyper_ref.7, bf16[1024,1024]{1,0:T(8,128)(2,1)} %get-tuple-element.85.dg_ref, bf16[1024,1024]{1,0:T(8,128)(2,1)} %get-tuple-element.86.du_ref, bf16[2048,1024]{1,0:T(8,128)(2,1)} %all-gather.4.cloned.1.call-done.wg_hbm.wg, ...), custom_call_target="tpu_custom_call" | custom-call | flops 49999998976 | bytes 8000000 | tf_op jit(solution)/shard_map/second/pallas_call | solution.py:948
  423.3 56.1 %attention_back.1 = (bf16[1024,256]{1,0:T(8,128)(2,1)}, bf16[1024,256]{1,0:T(8,128)(2,1)}, bf16[1024,256]{1,0:T(8,128)(2,1)}, f32[1024,256]{1,0:T(8,128)}) custom-call(bf16[1024,2048]{1,0:T(8,128)(2,1)} %get-tuple-element.107.one_ref, bf16[256,2048]{1,0:T(8,128)(2,1)} %get-tuple-element.77.wo_ref, bf16[1024,256]{1,0:T(8,128)(2,1)} %get-tuple-element.91.q_ref, ...), custom_call_target="tpu_custom_call" | custom-call | flops 49999998976 | bytes 8000000 | tf_op jit(solution)/shard_map/attention_back/pallas_call | solution.py:948
  479.4 2.9 convert_element_type.51
  482.3 2.8 convert_element_type.52
  485.1 2.8 convert_element_type.53
  487.9 4.5 convolution_convert_fusion.6
  492.4 4.6 convolution_convert_fusion.5
  497.0 4.6 convolution_convert_fusion.4
  501.6 4.5 convolution_convert_fusion.3
  506.2 0.7 reduce-scatter.16.cloned.1.call-update
  507.0 0.7 reduce-scatter.18.cloned.1.call-update
  507.7 0.2 slice_reduce_fusion.4
  508.0 0.3 reduce-scatter.20.cloned.1.call-update
  508.2 51.2 %last.1.d1_ref = f32[1024,256]{1,0:T(8,128)} custom-call(bf16[1024,256]{1,0:T(8,128)(2,1)} %get-tuple-element.108.dq_ref, bf16[1024,256]{1,0:T(8,128)(2,1)} %get-tuple-element.109.dk_ref, bf16[1024,256]{1,0:T(8,128)(2,1)} %get-tuple-element.110.dv_ref, bf16[2048,256]{1,0:T(8,128)(2,1)} %get-tuple-element.72.wq, bf16[2048,256]{1,0:T(8,128)(2,1)} %get-tuple-element.73.wk, ...), custom_call_target="tpu_custom_call" | custom-call | flops 49999998976 | bytes 8000000 | tf_op jit(solution)/shard_map/last/pallas_call | solution.py:948
  559.5 2.2 copy-done.1
  561.7 2.2 copy-done.3
  563.9 1.2 copy-done.4
  565.1 1.3 copy-done.5
  566.4 1.3 copy-done.6
  567.7 1.2 copy-done.7
  568.9 7.8 %leave.1 = (f32[4,1024,256]{2,1,0:T(8,128)}, f32[4,1024,256]{2,1,0:T(8,128)}, f32[17,8,128]{2,1,0:T(8,128)S(1)}) custom-call(f32[2,4,6]{2,1,0:T(4,128)S(1)} %copy-done.9, f32[4,1024,256]{2,1,0:T(8,128)S(1)} %copy-done.1, f32[4,1024,256]{2,1,0:T(8,128)S(1)} %copy-done.3, f32[1024,256]{1,0:T(8,128)S(1)} %copy-done.4, f32[1024,256]{1,0:T(8,128)S(1)} %copy-done.6, ...), custom_call_target="tpu_custom_call" | custom-call | flops 1000000000 | bytes 20000000 | tf_op jit(solution)/shard_map/leave/pallas_call | solution.py:981
  576.7 0.6 copy-done.14
  577.4 11.9 %totals.1 = (f32[40,128]{1,0:T(8,128)}, f32[8,128]{1,0:T(8,128)}) custom-call(f32[16,8,128]{2,1,0:T(8,128)} %copy-done.15, f32[17,8,128]{2,1,0:T(8,128)} %copy-done.14, f32[8,128]{1,0:T(8,128)} %get-tuple-element.124.top_ref), custom_call_target="tpu_custom_call" | custom-call | flops 49999998976 | bytes 8000000 | tf_op jit(solution)/shard_map/totals/pallas_call | solution.py:948
  589.3 1.2 slice.50
  590.5 0.8 slice_reduce_fusion
  591.5 0.9 slice_reduce_fusion.1
  592.4 0.2 multiply_reduce_fusion.3
  592.6 0.1 copy.32
  592.7 0.1 copy.34
  592.8 0.7 bitcast_add_fusion.1
  593.7 0.6 pad_maximum_fusion.2
  594.3 0.8 sqrt_reduce_fusion
  595.1 1.0 convert_multiply_fusion
  596.2 1.8 convert_element_type.58
  598.0 1.8 convert_element_type.59
  599.8 1.8 convert_element_type.60
  601.5 10.4 %reduce-scatter.20.cloned.1.call-done = bf16[256,512]{1,0:T(8,128)(2,1)} async-done(((bf16[256,2048]{1,0:T(8,128)(2,1)}), bf16[256,512]{1,0:T(8,128)(2,1)}) %reduce-scatter.20.cloned.1.call-update) | async-done | bytes 262160 | tf_op jit(solution)/shard_map/reduce_scatter | solution.py:998
  611.9 1.8 convert_element_type.61
  (70 shorter events, 1.2 us)
Async XLA Ops:
  7.2 156.0 %all-gather.4.cloned.1.call-start = ((), (), s32[]{:S(2)}) async-start(), calls=%async_computation.7 | async-start | bytes 5242880 | tf_op jit(solution)/shard_map/all_gather | solution.py:1040
  7.9 155.3 %all-gather.6.cloned.1.call-start = ((), (), s32[]{:S(2)}) async-start(), calls=%async_computation.8 | async-start | bytes 5242880 | tf_op jit(solution)/shard_map/all_gather | solution.py:1041
  8.7 154.5 %all-gather.8.cloned.1.call-start = ((), (), s32[]{:S(2)}) async-start(), calls=%async_computation.9 | async-start | bytes 5242880 | tf_op jit(solution)/shard_map/all_gather | solution.py:1042
  9.4 470.0 %reduce-scatter.8.cloned.1.call-start = ((), (), s32[]{:S(2)}) async-start(), calls=%async_computation.10 | async-start | bytes 5242880 | tf_op jit(solution)/shard_map/reduce_scatter | solution.py:998
  9.4 2.2 copy-start
  11.6 2.2 copy-start.2
  13.8 0.7 copy-start.8
  18.5 1.0 copy-start.10
  19.4 1.0 copy-start.11
  20.4 1.0 copy-start.12
  21.4 0.8 copy-start.13
  22.2 0.6 copy-start.15
  22.8 75.2 %copy-start.19 = (s32[1,2]{1,0:T(1,128)S(1)}, s32[1,2]{1,0:T(1,128)}, u32[]{:S(2)}) copy-start(s32[1,2]{1,0:T(1,128)} %param.24) | copy-start | bytes 28
  22.8 75.2 %copy-start.20 = (s32[1,2]{1,0:T(1,128)S(1)}, s32[1,2]{1,0:T(1,128)}, u32[]{:S(2)}) copy-start(s32[1,2]{1,0:T(1,128)} %param.25) | copy-start | bytes 28
  22.8 78.6 %copy-start.18 = (s32[1,1024]{1,0:T(1,128)S(1)}, s32[1,1024]{1,0:T(1,128)}, u32[]{:S(2)}) copy-start(s32[1,1024]{1,0:T(1,128)} %param.23) | copy-start | bytes 12292
  287.5 9.5 %copy-start.26 = (bf16[1024,1024]{1,0:T(8,128)(2,1)S(1)}, bf16[1024,1024]{1,0:T(8,128)(2,1)}, u32[]{:S(2)}) copy-start(bf16[1024,1024]{1,0:T(8,128)(2,1)} %get-tuple-element.85.dg_ref) | copy-start | bytes 6291460
  315.2 167.1 %reduce-scatter.10.cloned.1.call-start = ((), (), s32[]{:S(2)}) async-start(), calls=%async_computation.11 | async-start | bytes 5242880 | tf_op jit(solution)/shard_map/reduce_scatter | solution.py:998
  315.8 169.3 %reduce-scatter.12.cloned.1.call-start = ((), (), s32[]{:S(2)}) async-start(), calls=%async_computation.12 | async-start | bytes 5242880 | tf_op jit(solution)/shard_map/reduce_scatter | solution.py:998
  316.3 279.8 %reduce-scatter.14.cloned.1.call-start = ((), (), s32[]{:S(2)}) async-start(), calls=%async_computation.13 | async-start | bytes 1310720 | tf_op jit(solution)/shard_map/reduce_scatter | solution.py:998
  479.4 8.5 %copy-start.22 = (bf16[1024,256]{1,0:T(8,128)(2,1)S(1)}, bf16[1024,256]{1,0:T(8,128)(2,1)}, u32[]{:S(2)}) copy-start(bf16[1024,256]{1,0:T(8,128)(2,1)} %get-tuple-element.76.att_ref) | copy-start | bytes 1572868
  487.9 4.5 copy-start.23
  492.4 4.6 copy-start.24
  497.0 4.6 copy-start.25
  501.6 6.1 copy-start.9
  506.2 91.8 %reduce-scatter.16.cloned.1.call-start = ((), (), s32[]{:S(2)}) async-start(), calls=%async_computation.14 | async-start | bytes 1310720 | tf_op jit(solution)/shard_map/reduce_scatter | solution.py:998
  506.9 92.8 %reduce-scatter.18.cloned.1.call-start = ((), (), s32[]{:S(2)}) async-start(), calls=%async_computation.15 | async-start | bytes 1310720 | tf_op jit(solution)/shard_map/reduce_scatter | solution.py:998
  507.6 104.3 %reduce-scatter.20.cloned.1.call-start = ((), (), s32[]{:S(2)}) async-start(), calls=%async_computation.16 | async-start | bytes 1310720 | tf_op jit(solution)/shard_map/reduce_scatter | solution.py:998
  559.5 2.2 copy-start.1
  561.7 2.2 copy-start.3
  563.9 1.3 copy-start.4
  565.1 1.3 copy-start.5
  566.4 1.3 copy-start.6
  567.7 1.2 copy-start.7
  576.7 0.6 copy-start.14
  577.4 17.8 %copy-start.16 = (bf16[512,256]{1,0:T(8,128)(2,1)S(1)}, bf16[512,256]{1,0:T(8,128)(2,1)}, u32[]{:S(2)}) copy-start(bf16[512,256]{1,0:T(8,128)(2,1)} %sq.1) | copy-start | bytes 786436
  577.4 17.8 %copy-start.17 = (bf16[512,256]{1,0:T(8,128)(2,1)S(1)}, bf16[512,256]{1,0:T(8,128)(2,1)}, u32[]{:S(2)}) copy-start(bf16[512,256]{1,0:T(8,128)(2,1)} %sk.1) | copy-start | bytes 786436
  595.1 18.7 %copy-start.21 = (f32[2]{0:T(128)}, f32[2]{0:T(128)S(1)}, u32[]{:S(2)}) copy-start(f32[2]{0:T(128)S(1)} %sqrt_reduce_fusion) | copy-start | bytes 28
Sparse Core Ops, SparseCore 0:
  9.5 49.8 all-gather.3
  61.0 37.9 all-gather.5
  100.5 34.4 all-gather.7
  315.3 42.9 reduce-scatter.7
  361.2 44.6 reduce-scatter.9
  408.8 44.5 reduce-scatter.11
  506.3 22.6 reduce-scatter.13
  531.5 24.8 reduce-scatter.15
  558.9 25.5 reduce-scatter.17
  586.8 25.0 reduce-scatter.19

commit v3 on v2

--- a/solution.py
+++ b/solution.py
@@ -126,8 +126,9 @@
     def place_own(self):
         self.g_ref[:, pl.ds(pl.multiple_of(self.w * self.bw, self.bw), self.bw)] = self.x_ref[...]
 
-    def step(self, s):
-        for c in range(self.chunks):
+    def step(self, s, part=0, parts=1):
+        size = self.chunks // parts
+        for c in range(part * size, (part + 1) * size):
 
             @pl.when(self.z - s >= 0)
             def _():
@@ -332,16 +333,25 @@
                 def _():
                     self.down(zd, c).wait_send()
 
-    def run(self):
+    def run(self, work=()):
+        work = list(work)
         self.begin(0)
-
-        def body(c, carry):
-            self.begin(c + 1)
-            self.relay(c)
-            return carry
-
-        lax.fori_loop(0, self.chunks - 1, body, 0)
-        self.relay(self.chunks - 1)
+        if work:
+            for c in range(self.chunks):
+                if c + 1 < self.chunks:
+                    self.begin(c + 1)
+                for item in work[c :: self.chunks]:
+                    item()
+                self.relay(c)
+        else:
+
+            def body(c, carry):
+                self.begin(c + 1)
+                self.relay(c)
+                return carry
+
+            lax.fori_loop(0, self.chunks - 1, body, 0)
+            self.relay(self.chunks - 1)
         for c in range(self.chunks):
             self.finish(c)
 
@@ -468,6 +478,122 @@
             self.onward(n, k).wait_send()
 
 
+class Reduce:
+    def __init__(self, groups, axis, lhs, rhs, outs, scratch):
+        d = lax.axis_index("dp")
+        self.x, self.core, self.chips = d // 2, d % 2, groups // 2
+        self.axis, self.lhs, self.rhs, self.outs = axis, lhs, rhs, outs
+        self.turned, self.snd, self.rcv, self.xs, self.xr, self.s_s, self.s_r, self.x_s, self.x_r = scratch
+        self.rows, self.width = outs[0].shape
+        self.tile = min(256, self.width)
+        if axis == 1:
+            self.turned[...] = jnp.transpose(lhs[...])
+
+    @staticmethod
+    def scratch(groups, axis, lhs, outs):
+        chips = groups // 2
+        rows, width = outs[0].shape
+        v, n = pltpu.VMEM, len(outs)
+        return [
+            v((rows, lhs.shape[0]), BF),
+            v((n, chips, rows, width), BF),
+            v((n, chips, rows, width), BF),
+            v((n, chips - 1, rows, width), BF),
+            v((n, chips - 1, rows, width), BF),
+            dma(n, chips),
+            dma(n, chips),
+            dma(n, chips - 1),
+            dma(n, chips - 1),
+        ]
+
+    def greet(self, sem):
+        pl.semaphore_signal(sem, 1, device_id={"dp": self.x * 2 + 1 - self.core})
+        for k in range(1, self.chips):
+            pl.semaphore_signal(sem, 1, device_id={"dp": (self.x + k) % self.chips * 2 + self.core})
+        return self.chips
+
+    def prepare(self, d):
+        if self.axis == 0:
+            self.turned[...] = jnp.transpose(self.lhs[:, pl.ds(pl.multiple_of(d * self.rows, self.rows), self.rows)])
+
+    def product(self, n, d, j):
+        start = j * self.tile if self.axis == 0 else d * self.width + j * self.tile
+        return mm(self.turned[...], self.rhs[n][:, pl.ds(pl.multiple_of(start, self.tile), self.tile)])
+
+    def cols(self, j):
+        return pl.ds(pl.multiple_of(j * self.tile, self.tile), self.tile)
+
+    def tiles(self, body):
+        def loop(j, carry):
+            body(j)
+            return carry
+
+        lax.fori_loop(0, self.width // self.tile, loop, 0)
+
+    def across(self, n, k):
+        other = self.x * 2 + 1 - self.core
+        return pltpu.make_async_remote_copy(
+            self.snd.at[n, k], self.rcv.at[n, k], self.s_s.at[n, k], self.s_r.at[n, k], device_id={"dp": other}
+        )
+
+    def along(self, n, k):
+        target = (self.x + k) % self.chips * 2 + self.core
+        return pltpu.make_async_remote_copy(
+            self.xs.at[n, k - 1],
+            self.xr.at[n, k - 1],
+            self.x_s.at[n, k - 1],
+            self.x_r.at[n, k - 1],
+            device_id={"dp": target},
+        )
+
+    def give(self, k):
+        d = (self.x + k) % self.chips * 2 + 1 - self.core
+        self.prepare(d)
+        for n in range(len(self.outs)):
+
+            def body(j):
+                self.snd[n, k, :, self.cols(j)] = self.product(n, d, j).astype(BF)
+
+            self.tiles(body)
+            self.across(n, k).start()
+
+    def take(self, k):
+        d = (self.x + k) % self.chips * 2 + self.core
+        self.prepare(d)
+        for n in range(len(self.outs)):
+            self.across(n, k).wait_recv()
+
+            def body(j):
+                total = self.product(n, d, j) + self.rcv[n, k, :, self.cols(j)].astype(F32)
+                if k == 0:
+                    self.outs[n][:, self.cols(j)] = total
+                else:
+                    self.xs[n, k - 1, :, self.cols(j)] = total.astype(BF)
+
+            self.tiles(body)
+            if k > 0:
+                self.along(n, k).start()
+
+    def work(self):
+        order = list(range(1, self.chips)) + [0]
+        return [partial(self.give, k) for k in order] + [partial(self.take, k) for k in order]
+
+    def finish(self):
+        for n in range(len(self.outs)):
+            for k in range(1, self.chips):
+                self.along(n, k).wait_recv()
+
+                def body(j):
+                    self.outs[n][:, self.cols(j)] += self.xr[n, k - 1, :, self.cols(j)].astype(F32)
+
+                self.tiles(body)
+        for n in range(len(self.outs)):
+            for k in range(self.chips):
+                self.across(n, k).wait_send()
+                if k > 0:
+                    self.along(n, k).wait_send()
+
+
 def tile_columns(block, bw):
     return jnp.concatenate([block] * (bw // 128), axis=1)
 
@@ -670,13 +796,13 @@
     for c in range(chunks):
         gather.begin(c)
     gather.place_own()
+    gather.step(1)
+    gather.step(2)
     for n in range(2):
         spread.hand_over(n)
-    gather.step(1)
+    gather.step(3)
     for n in range(2, 4):
         spread.hand_over(n)
-    gather.step(2)
-    gather.step(3)
     for zs in range(NZ):
         gather.got_side(zs)
     for n in range(4):
@@ -756,20 +882,28 @@
     length, width = q_ref.shape
     heads = width // HD
     top_ref[...] = jnp.full(top_ref.shape, MASKED, F32)
-    v_ref[...] = mm(x_ref[...], wv[...]).astype(BF)
-    for target, weight in ((q_ref, wq), (k_ref, wk)):
-        for h in range(heads):
-            cols = slice(h * HD, (h + 1) * HD)
-            raw = mm(x_ref[...], weight[:, cols])
-            target[:, cols] = turn(raw, cos_ref[...], sin_ref[...]).astype(BF)
-    gather.step(1)
     masks = (doc_c, doc_r, lab_c, lab_r)
-    todo = [(h, r0) for h in range(heads) for r0 in range(0, length, QB)]
-    for n, (h, r0) in enumerate(todo):
-        attention_rows(h, r0, scale, length, q_ref, k_ref, v_ref, o_ref, lse_ref, top_ref, masks)
-        if n == len(todo) // 2 - 1:
-            gather.step(2)
-    gather.step(3)
+
+    def project(h, target, weight):
+        cols = slice(h * HD, (h + 1) * HD)
+        raw = mm(x_ref[...], weight[:, cols])
+        target[:, cols] = turn(raw, cos_ref[...], sin_ref[...]).astype(BF)
+
+    def value():
+        v_ref[...] = mm(x_ref[...], wv[...]).astype(BF)
+
+    units = [value]
+    units += [partial(project, h, *pair) for pair in ((q_ref, wq), (k_ref, wk)) for h in range(heads)]
+    units += [
+        partial(attention_rows, h, r0, scale, length, q_ref, k_ref, v_ref, o_ref, lse_ref, top_ref, masks)
+        for h in range(heads)
+        for r0 in range(0, length, QB)
+    ]
+    steps = [partial(gather.step, n, part, 4) for n in range(1, NZ) for part in range(4)]
+    for n, unit in enumerate(units):
+        unit()
+        for step in steps[n * len(steps) // len(units) : (n + 1) * len(steps) // len(units)]:
+            step()
     for zs in range(NZ):
         gather.got_side(zs)
     gather.drain()
@@ -843,18 +977,22 @@
     gather.drain()
 
 
-def second_kernel(count, g_chunks, s_chunks, hyper_ref, dg_ref, du_ref, wg, wu, n_ref, i_ref, cd_ref,
-                  d2_ref, one_ref, sum_ref, x_ref, *rest):
+def second_kernel(count, groups, g_chunks, s_chunks, hyper_ref, dg_ref, du_ref, wg, wu, n_ref, i_ref, cd_ref, x2_ref,
+                  d2_ref, one_ref, gg_ref, gu_ref, sum_ref, x_ref, *rest):
     pos = place(count)
-    greet(pos[0], count)
+    reduce = Reduce(groups, 0, x2_ref, (dg_ref, du_ref), (gg_ref, gu_ref), rest[:9])
+    rest = rest[9:]
+    greet(pos[0], count, reduce)
 
     def part(rows, block):
         return mm_t(dg_ref[rows, :], block_rows(wg, block, count)) + mm_t(
             du_ref[rows, :], block_rows(wu, block, count)
         )
 
+    work = reduce.work()
+    now, later = work[: groups // 2 + 1], work[groups // 2 + 1 :]
     scatter = Scatter(pos, count, s_chunks, part, sum_ref, rest[:13])
-    scatter.run()
+    scatter.run(now)
     totals = Totals(pos, count, *rest[13:17])
     denormalize(pos, count, sum_ref, n_ref, i_ref, d2_ref, totals)
     x_ref[...] = (cd_ref[...] + joint(hyper_ref) * d2_ref[...]).astype(BF)
@@ -862,7 +1000,14 @@
     for c in range(g_chunks):
         gather.begin(c)
     gather.place_own()
-    gather.rest()
+    gather.step(1)
+    for item in later:
+        item()
+    gather.step(2)
+    gather.step(3)
+    reduce.finish()
+    for zs in range(NZ):
+        gather.got_side(zs)
     scatter.drain()
     gather.drain()
 
@@ -886,11 +1031,13 @@
     dv_acc[low:high, cols] += t_mm(weights.astype(BF), do)
 
 
-def attention_back_kernel(count, s_chunks, scale, one_ref, wo_ref, q_ref, k_ref, v_ref, lse_ref, cos_ref, sin_ref,
-                          doc_c, doc_r, lab_c, lab_r, hid_ref, wd_ref,
-                          dq_ref, dk_ref, dv_ref, b2_ref, do_ref, dq_acc, dk_acc, dv_acc, *scratch):
+def attention_back_kernel(count, groups, s_chunks, scale, one_ref, wo_ref, q_ref, k_ref, v_ref, lse_ref, cos_ref, sin_ref,
+                          doc_c, doc_r, lab_c, lab_r, hid_ref, wd_ref, two_ref,
+                          dq_ref, dk_ref, dv_ref, b2_ref, gd_ref, do_ref, dq_acc, dk_acc, dv_acc, *scratch):
     pos = place(count)
-    greet(pos[0], count)
+    reduce = Reduce(groups, 1, hid_ref, (two_ref,), (gd_ref,), scratch[:9])
+    scratch = scratch[9:]
+    greet(pos[0], count, reduce)
 
     def part(rows, block):
         return mm(hid_ref[rows, :], block_columns(wd_ref, slice(None), block, count))
@@ -904,11 +1051,14 @@
     dv_acc[...] = jnp.zeros_like(dv_acc)
     masks = (doc_c, doc_r, lab_c, lab_r)
     todo = [(h, r0) for h in range(heads) for r0 in range(0, length, QB)]
+    work = reduce.work()
     for n, (h, r0) in enumerate(todo):
         if n * s_chunks % len(todo) == 0 or s_chunks > len(todo):
             c = n * s_chunks // len(todo)
             if c + 1 < s_chunks:
                 scatter.begin(c + 1)
+            for item in work[c::s_chunks]:
+                item()
             scatter.relay(c)
         back_rows(h, r0, scale, length, q_ref, k_ref, v_ref, do_ref, lse_ref, dq_acc, dk_acc, dv_acc, masks)
     for h in range(heads):
@@ -918,12 +1068,17 @@
     dv_ref[...] = dv_acc[...].astype(BF)
     for c in range(s_chunks):
         scatter.finish(c)
+    reduce.finish()
     scatter.drain()
 
 
-def last_kernel(count, s_chunks, dq_ref, dk_ref, dv_ref, wq, wk, wv, n_ref, i_ref, d1_ref, sum_ref, *rest):
+def last_kernel(count, groups, s_chunks, dq_ref, dk_ref, dv_ref, wq, wk, wv, n_ref, i_ref, x1_ref, att_ref, one_ref,
+                d1_ref, gq_ref, gk_ref, gv_ref, go_ref, sum_ref, *rest):
     pos = place(count)
-    greet(pos[0], count)
+    reduce = Reduce(groups, 0, x1_ref, (dq_ref, dk_ref, dv_ref), (gq_ref, gk_ref, gv_ref), rest[:9])
+    reduce_out = Reduce(groups, 1, att_ref, (one_ref,), (go_ref,), rest[9:18])
+    rest = rest[18:]
+    greet(pos[0], count, reduce)
 
     def part(rows, block):
         return (
@@ -932,10 +1087,13 @@
             + mm_t(dv_ref[rows, :], block_rows(wv, block, count))
         )
 
+    work, work_out = reduce.work(), reduce_out.work()
     scatter = Scatter(pos, count, s_chunks, part, sum_ref, rest[:13])
-    scatter.run()
+    scatter.run(work[: groups // 2] + work_out[: groups // 2] + work[groups // 2 :] + work_out[groups // 2 :])
     totals = Totals(pos, count, *rest[13:])
     denormalize(pos, count, sum_ref, n_ref, i_ref, d1_ref, totals)
+    reduce.finish()
+    reduce_out.finish()
     scatter.drain()
 
 
@@ -984,18 +1142,10 @@
         out_shape=outs,
         in_specs=[SM] + [spec(a) for a in ins],
         out_specs=tuple(spec(a) for a in outs),
-        compiler_params=pltpu.CompilerParams(vmem_limit_bytes=32 * 1024 * 1024),
+        compiler_params=pltpu.CompilerParams(vmem_limit_bytes=60 * 1024 * 1024),
         name=name,
         cost_estimate=pl.CostEstimate(flops=1_000_000_000, bytes_accessed=20_000_000, transcendentals=0),
     )(hyper, *ins)
-
-
-def weight_sum(left, right):
-    return lax.dot_general(left, right, (((0,), (0,)), ((), ())), preferred_element_type=F32).astype(BF)
-
-
-def weight_shard(value, axis):
-    return lax.psum_scatter(value, "dp", scatter_dimension=axis, tiled=True).astype(F32)
 
 
 def hyper_grad(hyper, v):
@@ -1093,62 +1243,39 @@
         "middle",
         [SM, VM, VM, VM, ANY, ANY, ANY, ANY],
     )
-    down_sum, gate_sum, up_sum = (
-        weight_sum(hidden, two_grad),
-        weight_sum(x_two, gate_grad),
-        weight_sum(x_two, up_grad),
-    )
-    gate_grad, up_grad, hidden, down_sum, gate_sum, up_sum = lax.optimization_barrier(
-        (gate_grad, up_grad, hidden, down_sum, gate_sum, up_sum)
-    )
-    down_shard, gate_shard, up_shard = (
-        weight_shard(down_sum, 1),
-        weight_shard(gate_sum, 0),
-        weight_shard(up_sum, 0),
-    )
-    h_two_grad, one_grad = call(
-        partial(second_kernel, count, AG_CHUNKS, RS_CHUNKS),
+    wide_grad = shape(F32, *w_gate.shape)
+    h_two_grad, one_grad, gate_shard, up_shard = call(
+        partial(second_kernel, count, groups, AG_CHUNKS, RS_CHUNKS),
         3,
-        (small, whole),
-        [hyper, gate_grad, up_grad, gate_w, up_w, kept_two, inverse_two, cot_one],
-        [v((tokens, bw), F32), v((tokens, bw), BF)] + scatter_scratch + total_scratch + gather_scratch,
+        (small, whole, wide_grad, wide_grad),
+        [hyper, gate_grad, up_grad, gate_w, up_w, kept_two, inverse_two, cot_one, x_two],
+        [v((tokens, bw), F32), v((tokens, bw), BF)]
+        + Reduce.scratch(groups, 0, x_two, (w_gate, w_up))
+        + scatter_scratch
+        + total_scratch
+        + gather_scratch,
         "second",
-        [SM] + [VM] * 7,
-    )
-    query_low, key_low, value_low, branch_two = call(
-        partial(attention_back_kernel, count, RS_CHUNKS, scale),
+        [SM] + [VM] * 8,
+    )
+    query_low, key_low, value_low, branch_two, down_shard = call(
+        partial(attention_back_kernel, count, groups, RS_CHUNKS, scale),
         4,
-        (low, low, low, small),
-        [one_grad, out_w, queries, keys, values, log_sums, cos, sin] + masks + [hidden, down_w],
-        [v((tokens, bw), BF)] + [v((tokens, bw), F32)] * 3 + scatter_scratch,
+        (low, low, low, small, shape(F32, *w_down.shape)),
+        [one_grad, out_w, queries, keys, values, log_sums, cos, sin] + masks + [hidden, down_w, two_grad],
+        [v((tokens, bw), BF)] + [v((tokens, bw), F32)] * 3 + Reduce.scratch(groups, 1, hidden, (w_down,)) + scatter_scratch,
         "attention_back",
     )
-    query_low, key_low, value_low, one_grad, down_shard, gate_shard, up_shard = lax.optimization_barrier(
-        (query_low, key_low, value_low, one_grad, down_shard, gate_shard, up_shard)
-    )
-    query_low, key_low, value_low, out_sum, query_sum, key_sum, value_sum = lax.optimization_barrier(
-        (
-            query_low,
-            key_low,
-            value_low,
-            weight_sum(attended, one_grad),
-            weight_sum(x_one, query_low),
-            weight_sum(x_one, key_low),
-            weight_sum(x_one, value_low),
-        )
-    )
-    out_shard, query_shard, key_shard, value_shard = (
-        weight_shard(out_sum, 1),
-        weight_shard(query_sum, 0),
-        weight_shard(key_sum, 0),
-        weight_shard(value_sum, 0),
-    )
-    h_one_grad = call(
-        partial(last_kernel, count, RS_CHUNKS),
+    narrow_grad = shape(F32, *w_query.shape)
+    h_one_grad, query_shard, key_shard, value_shard, out_shard = call(
+        partial(last_kernel, count, groups, RS_CHUNKS),
         5,
-        small,
-        [query_low, key_low, value_low, query_w, key_w, value_w, kept_one, inverse_one],
-        [v((tokens, bw), F32)] + scatter_scratch + total_scratch,
+        (small, narrow_grad, narrow_grad, narrow_grad, shape(F32, *w_out.shape)),
+        [query_low, key_low, value_low, query_w, key_w, value_w, kept_one, inverse_one, x_one, attended, one_grad],
+        [v((tokens, bw), F32)]
+        + Reduce.scratch(groups, 0, x_one, (w_query, w_key, w_value))
+        + Reduce.scratch(groups, 1, attended, (w_out,))
+        + scatter_scratch
+        + total_scratch,
         "last",
     )
     streams_shape = shape(F32, 4, tokens, bw)

time: 630 us -> 598 us (0.949)
  Pallas kernels: 496 us -> 547 us
  matrix products: 45.9 us -> 0 us
  other arithmetic: 22.5 us -> 7.88 us
  waiting for transfers between devices: 15.3 us -> 2.11 us
  local copies, waits for them, and re-layouts: 26.2 us -> 17.6 us
    dot_general x7 -> x0, matrix products: 45.9 us -> none  [weight_sum(): lax.dot_general(left, right, (((0,), (0,)), ((), ())), preferred_element_...]
    pallas_call x7, Pallas kernels: 484 us -> 527 us  [call(): pl.pallas_call(kernel, out_shape=outs, in_specs=specs or [VM] * len(ins),...]
    convert_element_type x7 -> x0, other arithmetic: 15.6 us -> none  [weight_shard(): lax.psum_scatter(value, 'dp', scatter_dimension=axis, tiled=True)]
    reduce_scatter x7 -> x0, waiting for transfers between devices: 10.4 us -> none  [weight_shard(): lax.psum_scatter(value, 'dp', scatter_dimension=axis, tiled=True)]
    unnamed x54 -> x39, local copies, waits for them, and re-layouts: 19.5 us -> 9.52 us
    pallas_call x2, Pallas kernels: 11.8 us -> 19.6 us  [rows_call(): pl.pallas_call(kernel, grid=(tokens // ROWS,), out_shape=outs, in_specs=[...]
  transfers between devices with their start and end apart: 10 -> 3, of which waited for: 1 -> 0; matrix products, arithmetic and copies ran while one was open for 4% -> 1% of each run, Pallas kernels for 60% -> 22%
where the time goes in v3:
time: 598 us; the launch traced here: 589 us
  Pallas kernels  547 us (91%)
  local copies, waits for them, and re-layouts  17.6 us (3%)
  between operations  14.5 us (2%)
  other arithmetic  7.88 us (1%)
    pallas_call x7, Pallas kernels, call(): pl.pallas_call(kernel, out_shape=outs, in_specs=specs or [VM] * len(ins),...  527 us
    pallas_call x2, Pallas kernels, rows_call(): pl.pallas_call(kernel, grid=(tokens // ROWS,), out_shape=outs, in_specs=[...  19.6 us
  transfers between devices with their start and end apart: 3, of which 0 were waited for; matrix products, arithmetic and copies ran while one was open for 1% of the time, Pallas kernels for 22%

profile of v3, /device:TPU:0, one launch (start us, length us, event | category | flops | bytes accessed | tf_op | source)
XLA Modules:
  0.0 589.2 jit_solution(6254189626557770872)
XLA Ops:
  7.2 0.0 all-gather.4.cloned.1.call-start
  7.2 0.7 all-gather.4.cloned.1.call-update
  7.9 0.0 all-gather.6.cloned.1.call-start
  8.0 0.7 all-gather.6.cloned.1.call-update
  8.7 0.0 all-gather.8.cloned.1.call-start
  8.7 0.7 all-gather.8.cloned.1.call-update
  9.4 7.8 %enter.1 = (f32[1024,256]{1,0:T(8,128)}, f32[1024,256]{1,0:T(8,128)}, f32[1024,256]{1,0:T(8,128)}, bf16[1024,256]{1,0:T(8,128)(2,1)}, f32[16,8,128]{2,1,0:T(8,128)}) custom-call(f32[2,4,6]{2,1,0:T(4,128)} %hyper_ref.7, f32[4,1024,256]{2,1,0:T(8,128)} %s_ref.3, f32[4,1024,256]{2,1,0:T(8,128)} %c_ref.3), custom_call_target="tpu_custom_call" | custom-call | flops 1000000000 | bytes 20000000 | tf_op jit(solution)/shard_map/enter/pallas_call | solution.py:1139
  17.2 0.0 copy-start.6
  17.2 0.0 copy-start.13
  17.3 0.0 copy-start.14
  17.3 0.0 copy-start.8
  17.3 67.0 %first.1 = (bf16[1024,2048]{1,0:T(8,128)(2,1)}, f32[1024,256]{1,0:T(8,128)}, f32[1024,128]{1,0:T(8,128)}, bf16[2048,256]{1,0:T(8,128)(2,1)}, bf16[2048,256]{1,0:...) custom-call(f32[1024,256]{1,0:T(8,128)} %get-tuple-element.58.h_ref, bf16[512,256]{1,0:T(8,128)(2,1)} %sq.1, ...), custom_call_target="tpu_custom_call" | custom-call | flops 49999998976 | bytes 8000000 | tf_op jit(solution)/shard_map/first/pallas_call | solution.py:1106
  84.3 0.0 copy-done.6
  84.3 0.8 slice_reduce_fusion.4
  85.1 0.0 copy-done.13
  85.1 0.0 copy-done.14
  85.1 0.1 fusion.2
  85.2 1.9 fusion
  87.1 1.3 pad_maximum_fusion
  88.4 0.7 slice_bitcast_fusion
  89.1 1.0 broadcast_in_dim.29.lab_c
  90.1 0.0 copy-done.8
  90.1 1.0 broadcast_in_dim.25.doc_c
  91.1 0.6 broadcast_in_dim.30.lab_r
  91.7 0.6 broadcast_in_dim.26.doc_r
  92.3 56.7 %attention.1 = (bf16[1024,256]{1,0:T(8,128)(2,1)}, bf16[1024,256]{1,0:T(8,128)(2,1)}, bf16[1024,256]{1,0:T(8,128)(2,1)}, bf16[1024,256]{1,0:T(8,128)(2,1)}, f32[...) custom-call(bf16[1024,2048]{1,0:T(8,128)(2,1)} %get-tuple-element.59.x_ref.x1_ref, ...), custom_call_target="tpu_custom_call" | custom-call | flops 49999998976 | bytes 8000000 | tf_op jit(solution)/shard_map/attention/pallas_call | solution.py:1106
  149.1 0.0 all-gather.4.cloned.1.call-done.wg_hbm.wg
  149.1 0.0 all-gather.6.cloned.1.call-done.wu_hbm.wu
  149.1 0.0 all-gather.8.cloned.1.call-done.wd_hbm.wd_ref
  149.1 125.4 %middle.1 = (f32[1024,256]{1,0:T(8,128)}, f32[1024,256]{1,0:T(8,128)}, f32[1024,128]{1,0:T(8,128)}, bf16[1024,2048]{1,0:T(8,128)(2,1)}, bf16[1024,1024]{1,0:T(8,...) custom-call(f32[2,4,6]{2,1,0:T(4,128)} %hyper_ref.7, bf16[1024,256]{1,0:T(8,128)(2,1)} %get-tuple-element.64.att_ref, ...), custom_call_target="tpu_custom_call" | custom-call | flops 49999998976 | bytes 8000000 | tf_op jit(solution)/shard_map/middle/pallas_call | solution.py:1106
  274.5 122.5 %second.1 = (f32[1024,256]{1,0:T(8,128)}, bf16[1024,2048]{1,0:T(8,128)(2,1)}, f32[512,1024]{1,0:T(8,128)}, f32[512,1024]{1,0:T(8,128)}) custom-call(f32[2,4,6]{2,1,0:T(4,128)} %hyper_ref.7, bf16[1024,1024]{1,0:T(8,128)(2,1)} %get-tuple-element.69.dg_ref, bf16[1024,1024]{1,0:T(8,128)(2,1)} %get-tuple-element.70.du_ref, ...), custom_call_target="tpu_custom_call" | custom-call | flops 49999998976 | bytes 8000000 | tf_op jit(solution)/shard_map/second/pallas_call | solution.py:1106
  397.0 67.3 %attention_back.1 = (bf16[1024,256]{1,0:T(8,128)(2,1)}, bf16[1024,256]{1,0:T(8,128)(2,1)}, bf16[1024,256]{1,0:T(8,128)(2,1)}, f32[1024,256]{1,0:T(8,128)}, f32[1024,512]{1,0:T(8,128)}) custom-call(bf16[1024,2048]{1,0:T(8,128)(2,1)} %get-tuple-element.75.one_ref, bf16[256,2048]{1,0:T(8,128)(2,1)} %get-tuple-element.65.wo_ref, ...), custom_call_target="tpu_custom_call" | custom-call | flops 49999998976 | bytes 8000000 | tf_op jit(solution)/shard_map/attention_back/pallas_call | solution.py:1106
  464.4 74.0 %last.1 = (f32[1024,256]{1,0:T(8,128)}, f32[512,256]{1,0:T(8,128)}, f32[512,256]{1,0:T(8,128)}, f32[512,256]{1,0:T(8,128)}, f32[256,512]{1,0:T(8,128)}) custom-call(bf16[1024,256]{1,0:T(8,128)(2,1)} %get-tuple-element.83.dq_ref, bf16[1024,256]{1,0:T(8,128)(2,1)} %get-tuple-element.84.dk_ref, bf16[1024,256]{1,0:T(8,128)(2,1)} %get-tuple-element.85.dv_ref, ...), custom_call_target="tpu_custom_call" | custom-call | flops 49999998976 | bytes 8000000 | tf_op jit(solution)/shard_map/last/pallas_call | solution.py:1106
  538.3 11.8 %leave.1 = (f32[4,1024,256]{2,1,0:T(8,128)}, f32[4,1024,256]{2,1,0:T(8,128)}, f32[17,8,128]{2,1,0:T(8,128)}) custom-call(f32[2,4,6]{2,1,0:T(4,128)} %hyper_ref.7, f32[4,1024,256]{2,1,0:T(8,128)} %s_ref.3, f32[4,1024,256]{2,1,0:T(8,128)} %c_ref.3, f32[1024,256]{1,0:T(8,128)} %get-tuple-element.68.b1_ref, f32[1024,256]{1,0:T(8,128)} %get-tuple-element.81.b2_ref, ...), custom_call_target="tpu_custom_call" | custom-call | flops 1000000000 | bytes 20000000 | tf_op jit(solution)/shard_map/leave/pallas_call | solution.py:1139
  550.1 0.0 copy-start.5
  550.1 0.0 copy-start.9
  550.2 0.0 copy-start.10
  550.2 0.0 copy-start.7
  550.2 0.0 copy-start.11
  550.2 14.5 %totals.1 = (f32[40,128]{1,0:T(8,128)}, f32[8,128]{1,0:T(8,128)}) custom-call(f32[16,8,128]{2,1,0:T(8,128)} %get-tuple-element.98.a_ref, f32[17,8,128]{2,1,0:T(8,128)} %get-tuple-element.99.b_ref, f32[8,128]{1,0:T(8,128)} %get-tuple-element.100.top_ref), custom_call_target="tpu_custom_call" | custom-call | flops 49999998976 | bytes 8000000 | tf_op jit(solution)/shard_map/totals/pallas_call | solution.py:1106
  564.7 1.0 slice_reduce_fusion
  565.7 0.9 slice_reduce_fusion.1
  566.6 1.2 slice.50
  567.8 0.8 sqrt_reduce_fusion
  568.6 0.0 copy-start.15
  568.6 0.1 broadcast_bitcast_fusion
  568.7 2.0 convert_multiply_fusion
  570.7 0.1 mul.162
  570.8 0.1 multiply_reduce_fusion.1
  570.9 0.0 copy-done.7
  570.9 0.2 multiply_reduce_fusion.3
  571.1 0.1 copy.32
  571.2 0.1 copy.34
  571.3 0.7 bitcast_add_fusion.1
  572.0 0.1 maximum_bitcast_fusion
  572.1 0.1 maximum_bitcast_fusion.1
  572.1 0.6 pad_maximum_fusion.2
  572.8 2.0 copy.43
  574.8 1.9 copy.44
  576.6 0.8 copy.45
  577.4 0.8 copy.46
  578.2 1.3 copy.47
  579.6 1.3 copy.48
  580.9 1.3 copy.49
  (20 shorter events, 0.1 us)
Async XLA Ops:
  7.2 141.9 %all-gather.4.cloned.1.call-start = ((), (), s32[]{:S(2)}) async-start(), calls=%async_computation | async-start | bytes 5242880 | tf_op jit(solution)/shard_map/all_gather | solution.py:1190
  7.9 141.2 %all-gather.6.cloned.1.call-start = ((), (), s32[]{:S(2)}) async-start(), calls=%async_computation.1 | async-start | bytes 5242880 | tf_op jit(solution)/shard_map/all_gather | solution.py:1191
  8.7 140.5 %all-gather.8.cloned.1.call-start = ((), (), s32[]{:S(2)}) async-start(), calls=%async_computation.2 | async-start | bytes 5242880 | tf_op jit(solution)/shard_map/all_gather | solution.py:1192
  17.2 67.1 %copy-start.6 = (f32[2,4,6]{2,1,0:T(4,128)S(1)}, f32[2,4,6]{2,1,0:T(4,128)}, u32[]{:S(2)}) copy-start(f32[2,4,6]{2,1,0:T(4,128)} %hyper_ref.7) | copy-start | bytes 580
  17.2 67.8 %copy-start.13 = (s32[1,2]{1,0:T(1,128)S(1)}, s32[1,2]{1,0:T(1,128)}, u32[]{:S(2)}) copy-start(s32[1,2]{1,0:T(1,128)} %param.24) | copy-start | bytes 28
  17.3 67.8 %copy-start.14 = (s32[1,2]{1,0:T(1,128)S(1)}, s32[1,2]{1,0:T(1,128)}, u32[]{:S(2)}) copy-start(s32[1,2]{1,0:T(1,128)} %param.25) | copy-start | bytes 28
  17.3 72.8 %copy-start.8 = (s32[1,1024]{1,0:T(1,128)S(1)}, s32[1,1024]{1,0:T(1,128)}, u32[]{:S(2)}) copy-start(s32[1,1024]{1,0:T(1,128)} %param.23) | copy-start | bytes 12292
  550.1 18.6 %copy-start.5 = (bf16[512,256]{1,0:T(8,128)(2,1)S(1)}, bf16[512,256]{1,0:T(8,128)(2,1)}, u32[]{:S(2)}) copy-start(bf16[512,256]{1,0:T(8,128)(2,1)} %sq.1) | copy-start | bytes 786436
  550.1 20.6 %copy-start.9 = (f32[4,4]{1,0:T(4,128)S(1)}, f32[4,4]{1,0:T(4,128)}, u32[]{:S(2)}) copy-start(f32[4,4]{1,0:T(4,128)} %get-tuple-element.115) | copy-start | bytes 196
  550.2 20.6 %copy-start.10 = (f32[4,4]{1,0:T(4,128)S(1)}, f32[4,4]{1,0:T(4,128)}, u32[]{:S(2)}) copy-start(f32[4,4]{1,0:T(4,128)} %get-tuple-element.116) | copy-start | bytes 196
  550.2 20.7 %copy-start.7 = (f32[2,4,6]{2,1,0:T(4,128)S(1)}, f32[2,4,6]{2,1,0:T(4,128)}, u32[]{:S(2)}) copy-start(f32[2,4,6]{2,1,0:T(4,128)} %hyper_ref.7) | copy-start | bytes 580
  550.2 20.7 %copy-start.11 = (f32[4]{0:T(128)S(1)}, f32[4]{0:T(128)}, u32[]{:S(2)}) copy-start(f32[4]{0:T(128)} %get-tuple-element.107) | copy-start | bytes 52
  550.2 20.7 %copy-start.12 = (f32[4]{0:T(128)S(1)}, f32[4]{0:T(128)}, u32[]{:S(2)}) copy-start(f32[4]{0:T(128)} %get-tuple-element.108) | copy-start | bytes 52
  550.2 26.4 %copy-start.4 = (f32[512,256]{1,0:T(8,128)S(1)}, f32[512,256]{1,0:T(8,128)}, u32[]{:S(2)}) copy-start(f32[512,256]{1,0:T(8,128)} %get-tuple-element.142) | copy-start | bytes 1572868
  564.7 12.7 %copy-start.3 = (f32[256,512]{1,0:T(8,128)S(1)}, f32[256,512]{1,0:T(8,128)}, u32[]{:S(2)}) copy-start(f32[256,512]{1,0:T(8,128)} %get-tuple-element.143) | copy-start | bytes 1572868
  564.7 13.5 %copy-start.1 = (f32[512,1024]{1,0:T(8,128)S(1)}, f32[512,1024]{1,0:T(8,128)}, u32[]{:S(2)}) copy-start(f32[512,1024]{1,0:T(8,128)} %get-tuple-element.144) | copy-start | bytes 6291460
  568.6 11.0 %copy-start.15 = (f32[2]{0:T(128)}, f32[2]{0:T(128)S(1)}, u32[]{:S(2)}) copy-start(f32[2]{0:T(128)S(1)} %sqrt_reduce_fusion) | copy-start | bytes 28
  572.8 6.8 %copy-start = (f32[512,1024]{1,0:T(8,128)S(1)}, f32[512,1024]{1,0:T(8,128)}, u32[]{:S(2)}) copy-start(f32[512,1024]{1,0:T(8,128)} %get-tuple-element.145) | copy-start | bytes 6291460
  578.2 2.6 copy-start.2
Sparse Core Ops, SparseCore 0:
  9.5 55.1 all-gather.3
  66.3 38.0 all-gather.5
  106.0 34.4 all-gather.7
